TPU v7x, 128 devices: a whole 4x4x4 slice. The times are simulated.
128 devices in a mesh: dom: 32 (over y, x, core), col: 4 (over z).
Axes of the slice: x: 4, y: 4, z: 4, core: 2. Of those that a mesh axis runs over, the one named last changes fastest.
Arguments:
- features: bfloat16 [262144, 1024], P('dom', 'col')
- weight: bfloat16 [1024, 1024], P(None, 'col'), may hold values from -0.1875 to 0.1875
- out_bias: bfloat16 [1024], P('col'), may hold values from -3 to 3
- local_index: int32 [32, 64, 4], P('dom'), may hold values from 0 to 63
- local_count: int32 [32, 64], P('dom'), may hold values from 1 to 4, as said below
- local_vals: bfloat16 [32, 64, 4, 128, 128], P('dom'), may hold values from -0.1875 to 0.1875
- halo_index: int32 [32, 64, 4], P('dom'), may hold values from 0 to 127
- halo_count: int32 [32, 64], P('dom'), may hold values from 0 to 4, as said below
- halo_vals: bfloat16 [32, 64, 4, 128, 128], P('dom'), may hold values from -0.1875 to 0.1875
- send_rows: int32 [32, 32, 512], P('dom'), may hold values from 0 to 8191
- send_count: int32 [32, 32], P('dom'), may hold values from 0 to 512, as said below
Outputs:
- normalized: bfloat16 [262144, 1024], P('dom', 'col')
- channel_stats: float32 [2, 1024], P(None, 'col')
Inputs may be any that keep to these rules, and one draw needn't show every extreme that they name: `local_index`: slots k >= local_count of a row tile are not used. `local_count`: every partition has a row tile with all 4 slots used. `halo_index`: slots k >= halo_count of a row tile are not used. `halo_count`: every partition has a row tile with all 4 slots used. `send_rows`: slots s >= send_count[q, p] are not used. send_count[p, p] is 0; every partition fills all 512 slots to some other partition.
All inputs are finite; a program needn't handle non-finite values.
Results may differ from a plain program's by a relative error of at most 0.0075.
Values may be sent and summed in bfloat16 or wider, within the bound.
A program may use at most 192 MiB of HBM per device.

v0:
```python
import functools

import jax
import jax.numpy as jnp
from jax import lax
from jax.sharding import Mesh
from jax.sharding import PartitionSpec as P

TILE = 128
DOM = ("dom_0", "dom_1", "dom_2")
DOM_COL = ("dom_0", "dom_1", "dom_2", "col")


epsilon = 1e-06


def from_everyone(value, axis):
    copies = jnp.broadcast_to(value, (lax.axis_size(axis), *value.shape))
    return lax.all_to_all(copies, axis, split_axis=0, concat_axis=0, tiled=True)


def joined_along(blocks, dim):
    shape = list(blocks.shape[1:])
    shape[dim] *= blocks.shape[0]
    return jnp.moveaxis(blocks, 0, dim).reshape(shape)


def collect(value, axis, dim):
    blocks = from_everyone(value, axis)
    return joined_along(blocks, dim)


def sent_together(arrays, axis, dim, along):
    both = jnp.concatenate(arrays, axis=along)
    result, at, done = (collect(both, axis, dim), 0, [])
    for a in arrays:
        done.append(lax.slice_in_dim(result, at, at + a.shape[along], axis=along))
        at += a.shape[along]
    return tuple(done)


def one_axis_at_a_time(value, axes):
    return functools.reduce(lax.psum, axes, value)


def tile_sum(sources, tile_index, tile_count, tile_vals):
    gathered = sources[tile_index]
    keep_mask = jnp.arange(tile_vals.shape[1])[None, :] < tile_count[:, None]
    masked = jnp.where(keep_mask[:, :, None, None], tile_vals, jnp.zeros_like(tile_vals))
    return jnp.einsum("tkij,tkjc->tic", masked, gathered, preferred_element_type=jnp.float32)


def on_device(
    features,
    weight,
    out_bias,
    local_index,
    local_count,
    local_vals,
    halo_index,
    halo_count,
    halo_vals,
    send_rows,
    send_count,
):
    row_count, col_width = features.shape
    peer_count = lax.axis_size(DOM)
    slot_total = send_rows.shape[2]
    chosen = features[send_rows[0]]
    keep_mask = jnp.arange(slot_total)[None, :] < send_count[0][:, None]
    outgoing = jnp.where(keep_mask[:, :, None], chosen, jnp.zeros_like(chosen))
    arrived = lax.all_to_all(outgoing, DOM, split_axis=0, concat_axis=0, tiled=True)
    halo_tiles = arrived.reshape(peer_count * slot_total // TILE, TILE, col_width)
    own_tiles = features.reshape(row_count // TILE, TILE, col_width)
    summed = tile_sum(own_tiles, local_index[0], local_count[0], local_vals[0])
    summed = summed + tile_sum(halo_tiles, halo_index[0], halo_count[0], halo_vals[0])
    spread = summed.reshape(row_count, col_width).astype(jnp.bfloat16)
    node_total = row_count * peer_count
    regrouped = lax.all_to_all(spread, "col", split_axis=0, concat_axis=1, tiled=True)
    full_weight, full_bias = sent_together((weight, out_bias.reshape(1, col_width)), "col", 1, 0)
    mixed_rows = jnp.dot(regrouped, full_weight, preferred_element_type=jnp.float32) + full_bias[
        0
    ].astype(jnp.float32)
    active = jnp.maximum(mixed_rows, 0.0)
    row_power = jnp.mean(active * active, axis=1, keepdims=True)
    scaled = active * lax.rsqrt(row_power + epsilon)
    sum_whole, square_whole = (
        one_axis_at_a_time(jnp.sum(scaled, axis=0), DOM_COL),
        one_axis_at_a_time(jnp.sum(scaled * scaled, axis=0), DOM_COL),
    )
    normalized = lax.all_to_all(
        scaled.astype(jnp.bfloat16), "col", split_axis=1, concat_axis=0, tiled=True
    )
    column_start = lax.axis_index("col") * col_width
    sum_total = lax.dynamic_slice_in_dim(sum_whole, column_start, col_width, 0)
    square_total = lax.dynamic_slice_in_dim(square_whole, column_start, col_width, 0)
    channel_mean = sum_total / node_total
    channel_var = square_total / node_total - channel_mean * channel_mean
    return (normalized, jnp.stack([channel_mean, channel_var]))


def solution(mesh):
    split = Mesh(
        mesh.devices.reshape(4, 4, 2, mesh.shape["col"]), ("dom_0", "dom_1", "dom_2", "col")
    )
    in_specs = (
        P(DOM, "col"),
        P(None, "col"),
        P("col"),
        P(DOM, None, None),
        P(DOM, None),
        P(DOM, None, None, None, None),
        P(DOM, None, None),
        P(DOM, None),
        P(DOM, None, None, None, None),
        P(DOM, None, None),
        P(DOM, None),
    )
    out_specs = (P(DOM, "col"), P(None, "col"))
    return jax.shard_map(
        on_device, mesh=split, in_specs=in_specs, out_specs=out_specs, check_vma=False
    )
```

profile of v0, /device:TPU:6, one launch (start us, length us, event | category | flops | bytes accessed | tf_op | source)
XLA Modules:
  0.0 365.2 jit_solution(15775442864130930582)
XLA Ops:
  0.6 0.8 fusion.10
  1.5 0.7 iota_compare_fusion
  2.3 63.5 %gather_fusion.1 = bf16[16384,256]{1,0:T(8,128)(2,1)} fusion(bf16[8192,256]{1,0:T(8,128)(2,1)} %param.11, s32[16384]{0:T(1024)S(1)} %broadcast_clamp_fusion), kind=kCustom, calls=%fused_computation.1 | custom fusion | bytes 16842752 | tf_op jit(solution)/shard_map/gather | solution.py:69
  65.8 8.1 %broadcast_select_fusion = bf16[32,512,256]{2,1,0:T(8,128)(2,1)} fusion(bf16[32,512,256]{2,1,0:T(8,128)(2,1)} %bitcast.58, pred[32,512]{1,0:T(8,128)(4,1)S(1)} %iota_compare_fusion), kind=kLoop, calls=%fused_computation.12 | loop fusion | flops 4194304 | bytes 16793600 | tf_op jit(solution)/shard_map/jit(_where)/select_n | solution.py:71
  73.9 7.8 %all-to-all-start = ((bf16[32,512,256]{2,1,0:T(8,128)(2,1)}), bf16[32,512,256]{2,1,0:T(8,128)(2,1)}, u32[]{:S(2)}, u32[]{:S(2)}) async-start(bf16[32,512,256]{2,1,0:T(8,128)(2,1)} %broadcast_select_fusion), calls=%async_computation | async-start | bytes 16777216 | tf_op jit(solution)/shard_map/all_to_all | solution.py:72
  81.7 0.1 copy.25
  81.8 0.1 reshape.219
  81.9 0.1 copy.24
  82.0 0.1 reshape.203
  82.2 12.0 %gather_fusion = bf16[256,128,256]{2,1,0:T(8,128)(2,1)} fusion(bf16[64,128,256]{2,1,0:T(8,128)(2,1)} %bitcast.55, s32[1024]{0:T(1024)S(1)} %pad_clamp_fusion.1), kind=kCustom, calls=%fused_computation | custom fusion | bytes 33555456 | tf_op jit(solution)/shard_map/gather | solution.py:47
  94.4 86.1 %all-to-all-done = bf16[32,512,256]{2,1,0:T(8,128)(2,1)} async-done(((bf16[32,512,256]{2,1,0:T(8,128)(2,1)}), bf16[32,512,256]{2,1,0:T(8,128)(2,1)}, u32[]{:S(2)}, u32[]{:S(2)}) %all-to-all-start) | async-done | bytes 8388640 | tf_op jit(solution)/shard_map/all_to_all | solution.py:72
  180.5 1.5 broadcast_in_dim.42
  182.0 5.3 %all-to-all-start.2 = ((bf16[4,1025,256]{2,1,0:T(8,128)(2,1)}), bf16[4,1025,256]{2,1,0:T(8,128)(2,1)S(1)}, u32[]{:S(2)}, u32[]{:S(2)}) async-start(bf16[4,1025,256]{2,1,0:T(8,128)(2,1)} %broadcast_in_dim.42), calls=%async_computation.2 | async-start | bytes 4227072 | tf_op jit(solution)/shard_map/all_to_all | solution.py:19
  187.3 13.1 %gather_fusion.2 = bf16[256,128,256]{2,1,0:T(8,128)(2,1)} fusion(bf16[128,128,256]{2,1,0:T(8,128)(2,1)} %bitcast.12, s32[1024]{0:T(1024)S(1)} %pad_clamp_fusion), kind=kCustom, calls=%fused_computation.2 | custom fusion | bytes 33555456 | tf_op jit(solution)/shard_map/gather | solution.py:47
  200.4 13.8 %fusion.1 = f32[64,128,256,1]{2,1,3,0:T(8,128)} fusion(bf16[64,4,128,256]{3,2,1,0:T(8,128)(2,1)} %bitcast.56, bf16[1,64,4,128,128]{4,3,2,1,0:T(8,128)(2,1)} %param.19, pred[64,4]{1,0:T(8,128)(4,1)S(1)} %iota_compare_fusion.1), kind=kOutput, calls=%fused_computation.6 | convolution fusion | flops 2151677952 | bytes 33554688 | tf_op jit(solution)/shard_map/tkij,tkjc->tic/dot_general | solution.py:50
  214.2 14.0 %fusion = bf16[64,128,256]{2,1,0:T(8,128)(2,1)} fusion(f32[64,128,256,1]{2,1,3,0:T(8,128)} %fusion.1, bf16[64,4,128,256]{3,2,1,0:T(8,128)(2,1)} %bitcast.57, bf16[1,64,4,128,128]{4,3,2,1,0:T(8,128)(2,1)} %param.16, pred[64,4]{1,0:T(8,128)(4,1)S(1)} %iota_compare_fusion.2), kind=kOutput, calls=%fused_computation.4 | convolution fusion | flops 2155872256 | bytes 37748992 | tf_op jit(solution)/shard_map/tkij,tkjc->tic/dot_general | solution.py:50
  228.2 6.3 %copy.26 = bf16[4,2048,256]{1,2,0:T(8,128)(2,1)} copy(bf16[4,2048,256]{2,1,0:T(8,128)(2,1)} %bitcast.59) | data formatting | bytes 8388608 | tf_op jit(solution)/shard_map/convert_element_type | solution.py:77
  234.4 1.3 copy-done
  235.8 5.0 %all-to-all-start.1 = ((bf16[4,2048,256]{1,2,0:T(8,128)(2,1)}), bf16[4,2048,256]{1,2,0:T(8,128)(2,1)}, u32[]{:S(2)}, u32[]{:S(2)}) async-start(bf16[4,2048,256]{1,2,0:T(8,128)(2,1)} %copy.26), calls=%async_computation.1 | async-start | bytes 8388608 | tf_op jit(solution)/shard_map/all_to_all | solution.py:79
  240.8 2.9 copy.27
  243.7 1.6 slice.19
  245.4 0.1 convert_reduce_fusion
  245.5 44.3 %all-to-all-done.1 = bf16[4,2048,256]{1,2,0:T(8,128)(2,1)} async-done(((bf16[4,2048,256]{1,2,0:T(8,128)(2,1)}), bf16[4,2048,256]{1,2,0:T(8,128)(2,1)}, u32[]{:S(2)}, u32[]{:S(2)}) %all-to-all-start.1) | async-done | bytes 4194336 | tf_op jit(solution)/shard_map/all_to_all | solution.py:79
  289.8 7.0 %multiply_reduce_fusion.1 = (f32[2048]{0:T(1024)S(1)}, f32[2048,1024]{0,1:T(8,128)S(1)}) fusion(f32[1024]{0:T(1024)S(1)} %bitcast.66, bf16[1024,1024]{0,1:T(8,128)(2,1)} %bitcast.64, bf16[2048,1024]{0,1:T(8,128)(2,1)} %bitcast.19), kind=kOutput, calls=%fused_computation.10 | convolution fusion | flops 4303353856 | bytes 14692352 | tf_op jit(solution)/shard_map/dot_general | solution.py:81
  296.8 3.5 fusion.6
  300.3 4.9 %all-to-all-start.3 = ((bf16[2048,4,256]{0,2,1:T(8,128)(2,1)}), bf16[2048,4,256]{0,2,1:T(8,128)(2,1)}, u32[]{:S(2)}, u32[]{:S(2)}) async-start(bf16[2048,4,256]{0,2,1:T(8,128)(2,1)} %bitcast.60), calls=%async_computation.3 | async-start | bytes 8388608 | tf_op jit(solution)/shard_map/all_to_all | solution.py:91
  305.2 8.7 %all-reduce.2 = (f32[1024]{0:T(1024)S(1)}, f32[1024]{0:T(1024)S(1)}) all-reduce(f32[1024]{0:T(1024)S(1)} %get-tuple-element.3, f32[1024]{0:T(1024)S(1)} %get-tuple-element.2), channel_id=1, replica_groups=mesh['dom_0'=4,'dom_1'=4,'dom_2'=2,'col'=4] {'dom_0'}, use_global_device_ids=true, to_apply=%region_7.8 | all-reduce | flops 2048 | bytes 16384 | tf_op jit(solution)/shard_map/psum | solution.py:43
  313.9 10.6 %all-reduce.1 = (f32[1024]{0:T(1024)S(1)}, f32[1024]{0:T(1024)S(1)}) all-reduce(f32[1024]{0:T(1024)S(1)} %get-tuple-element.8, f32[1024]{0:T(1024)S(1)} %get-tuple-element.9), channel_id=1, replica_groups=mesh['dom_0'=4,'dom_1'=4,'dom_2'=2,'col'=4] {'dom_1'}, use_global_device_ids=true, to_apply=%region_8.9 | all-reduce | flops 2048 | bytes 16384 | tf_op jit(solution)/shard_map/psum | solution.py:43
  324.6 2.5 all-reduce.3
  327.1 31.3 %all-reduce = (f32[1024]{0:T(1024)S(1)}, f32[1024]{0:T(1024)S(1)}) all-reduce(f32[1024]{0:T(1024)S(1)} %get-tuple-element.10, f32[1024]{0:T(1024)S(1)} %get-tuple-element.11), channel_id=1, replica_groups=mesh['dom_0'=4,'dom_1'=4,'dom_2'=2,'col'=4] {'col'}, use_global_device_ids=true, to_apply=%region_10.11 | all-reduce | flops 2048 | bytes 16384 | tf_op jit(solution)/shard_map/psum | solution.py:43
  358.4 0.6 pad_maximum_fusion.1
  359.0 6.2 %copy.28 = bf16[4,2048,256]{2,1,0:T(8,128)(2,1)} copy(bf16[4,2048,256]{1,2,0:T(8,128)(2,1)} %bitcast.23) | data formatting | bytes 8388608 | tf_op jit(solution)/shard_map/all_to_all | solution.py:91
  (28 shorter events, 0.4 us)
Async XLA Ops:
  73.9 7.8 %copy-start.6 = (bf16[256]{0:T(256)(128)(2,1)S(1)}, bf16[256]{0:T(256)(128)(2,1)}, u32[]{:S(2)}) copy-start(bf16[256]{0:T(256)(128)(2,1)} %param.13) | copy-start | bytes 1540
  73.9 7.8 %copy-start.2 = (s32[1,64,4]{1,2,0:T(4,128)S(1)}, s32[1,64,4]{1,2,0:T(4,128)}, u32[]{:S(2)}) copy-start(s32[1,64,4]{1,2,0:T(4,128)} %param.17) | copy-start | bytes 3076
  73.9 8.0 %copy-start.3 = (s32[1,64,4]{1,2,0:T(4,128)S(1)}, s32[1,64,4]{1,2,0:T(4,128)}, u32[]{:S(2)}) copy-start(s32[1,64,4]{1,2,0:T(4,128)} %param.14) | copy-start | bytes 3076
  73.9 106.6 %all-to-all-start = ((bf16[32,512,256]{2,1,0:T(8,128)(2,1)}), bf16[32,512,256]{2,1,0:T(8,128)(2,1)}, u32[]{:S(2)}, u32[]{:S(2)}) async-start(bf16[32,512,256]{2,1,0:T(8,128)(2,1)} %broadcast_select_fusion), calls=%async_computation | async-start | bytes 16777216 | tf_op jit(solution)/shard_map/all_to_all | solution.py:72
  82.1 12.0 %copy-start.4 = (s32[1,64]{1,0:T(1,128)S(1)}, s32[1,64]{1,0:T(1,128)}, u32[]{:S(2)}) copy-start(s32[1,64]{1,0:T(1,128)} %param.18) | copy-start | bytes 772
  82.1 12.1 %copy-start.5 = (s32[1,64]{1,0:T(1,128)S(1)}, s32[1,64]{1,0:T(1,128)}, u32[]{:S(2)}) copy-start(s32[1,64]{1,0:T(1,128)} %param.15) | copy-start | bytes 772
  82.2 12.2 %copy-start.1 = (bf16[1024,256]{1,0:T(8,128)(2,1)S(1)}, bf16[1024,256]{1,0:T(8,128)(2,1)}, u32[]{:S(2)}) copy-start(bf16[1024,256]{1,0:T(8,128)(2,1)} %param.12) | copy-start | bytes 1572868
  182.0 52.5 %all-to-all-start.2 = ((bf16[4,1025,256]{2,1,0:T(8,128)(2,1)}), bf16[4,1025,256]{2,1,0:T(8,128)(2,1)S(1)}, u32[]{:S(2)}, u32[]{:S(2)}) async-start(bf16[4,1025,256]{2,1,0:T(8,128)(2,1)} %broadcast_in_dim.42), calls=%async_computation.2 | async-start | bytes 4227072 | tf_op jit(solution)/shard_map/all_to_all | solution.py:19
  234.4 1.3 copy-start
  235.8 54.0 %all-to-all-start.1 = ((bf16[4,2048,256]{1,2,0:T(8,128)(2,1)}), bf16[4,2048,256]{1,2,0:T(8,128)(2,1)}, u32[]{:S(2)}, u32[]{:S(2)}) async-start(bf16[4,2048,256]{1,2,0:T(8,128)(2,1)} %copy.26), calls=%async_computation.1 | async-start | bytes 8388608 | tf_op jit(solution)/shard_map/all_to_all | solution.py:79
  300.3 58.7 %all-to-all-start.3 = ((bf16[2048,4,256]{0,2,1:T(8,128)(2,1)}), bf16[2048,4,256]{0,2,1:T(8,128)(2,1)}, u32[]{:S(2)}, u32[]{:S(2)}) async-start(bf16[2048,4,256]{0,2,1:T(8,128)(2,1)} %bitcast.60), calls=%async_computation.3 | async-start | bytes 8388608 | tf_op jit(solution)/shard_map/all_to_all | solution.py:91
where the time goes:
time: 366 us; the launch traced here: 365 us
  waiting for transfers between devices  130 us (36%)
  local copies, waits for them, and re-layouts  109 us (30%)
  blocking collectives  53.2 us (15%)
  matrix products  34.7 us (9%)
  starting transfers between devices  23 us (6%)
  other arithmetic  14.1 us (4%)
    all_to_all x1, waiting for transfers between devices, on_device(): lax.all_to_all(outgoing, DOM, split_axis=0, concat_axis=0, tiled=True)  86.1 us
    gather x1, local copies, waits for them, and re-layouts, on_device(): chosen = features[send_rows[0]]  63.5 us
    psum x4, blocking collectives, one_axis_at_a_time(): return functools.reduce(lax.psum, axes, value)  53.2 us
    all_to_all x1, waiting for transfers between devices, on_device(): lax.all_to_all(spread, 'col', split_axis=0, concat_axis=1, tiled=True)  44.3 us
    dot_general x2, matrix products, tile_sum(): jnp.einsum('tkij,tkjc->tic', masked, gathered, preferred_element_type=jnp...  27.7 us
    gather x2, local copies, waits for them, and re-layouts, tile_sum(): gathered = sources[tile_index]  25.1 us
    select_n x1, other arithmetic, on_device(): outgoing = jnp.where(keep_mask[:, :, None], chosen, jnp.zeros_like(chosen))  8.06 us
    all_to_all x1, starting transfers between devices, on_device(): lax.all_to_all(outgoing, DOM, split_axis=0, concat_axis=0, tiled=True)  7.76 us
  transfers between devices with their start and end apart: 4, of which 2 were waited for; matrix products, arithmetic and copies ran while one was open for 18% of the time, Pallas kernels for 0%

commit v1 on v0

v1 whole, which is shorter than its diff:
```python
import functools

import jax
import jax.numpy as jnp
from jax import lax
from jax.experimental import pallas as pl
from jax.experimental.pallas import tpu as pltpu
from jax.sharding import PartitionSpec as P

MESH = pl.DeviceIdType.MESH
epsilon = 1e-06

T = 128
HALF = 256
UNROLL = 32
ZORD = (2, 1, 3)
CH = 256
SLOTS = 4


def dom_of(y, x, c):
    return (y * 4 + x) * 2 + c


def layer(
    sidx, lidx, hidx, feat_hbm, w_hbm, bias_hbm, lval, hval,
    out, stats,
    feat, tab, stage, send, mid, recv, acc, abuf, spread, zrecv, wbuf, bbuf, nbuf,
    part, zst, xst, yst, cst,
    in_sem, a_sem, w_send, w_recv, b_send, b_recv,
    mid_send, mid_recv, dir_send, fwd_send, fin_recv,
    z_send, z_recv, o_send, o_recv, own_sem,
    sz_send, sz_recv, sx_send, sx_recv, sy_send, sy_recv, sc_send, sc_recv,
):
    d = lax.axis_index("dom")
    z = lax.axis_index("col")
    y, x, c = d // 8, (d // 2) % 4, d % 2

    def place(r, du, dv):
        if isinstance(r, int):
            return ((y + dv) % 4, (x + du) % 4) if r == 0 else ((y + du) % 4, (x + dv) % 4)
        dy = jnp.where(r == 0, dv, du)
        dx = jnp.where(r == 0, du, dv)
        return (y + dy) % 4, (x + dx) % 4

    def remote(src, dst, ssem, rsem, dom, col):
        return pltpu.make_async_remote_copy(
            src_ref=src, dst_ref=dst, send_sem=ssem, recv_sem=rsem,
            device_id={"dom": dom, "col": col}, device_id_type=MESH,
        )

    barrier = pltpu.get_barrier_semaphore()
    peers = []
    for k in range(1, 4):
        for cc in range(2):
            peers.append((dom_of(y, (x + k) % 4, cc), z))
            peers.append((dom_of((y + k) % 4, x, cc), z))
        peers.append((d, (z + k) % 4))
    peers.append((dom_of(y, x, 1 - c), z))
    for dom, col in peers:
        pl.semaphore_signal(
            barrier, inc=1, device_id={"dom": dom, "col": col}, device_id_type=MESH
        )

    feat_in = pltpu.make_async_copy(feat_hbm, feat.at[pl.ds(0, 64)], in_sem.at[0])
    feat_in.start()
    w_in = pltpu.make_async_copy(w_hbm, wbuf.at[z], in_sem.at[1])
    w_in.start()
    b_in = pltpu.make_async_copy(bias_hbm, bbuf.at[z], in_sem.at[2])
    b_in.start()

    def a_chunk(vals, chunk, slot):
        return pltpu.make_async_copy(vals.at[pl.ds(chunk * 2, 2)], abuf.at[slot], a_sem.at[slot])

    for s in range(SLOTS):
        a_chunk(lval, s, s).start()

    row = lax.broadcasted_iota(jnp.int32, (256, 256), 0)
    lane = lax.broadcasted_iota(jnp.int32, (256, 256), 1)
    split = jnp.where(lane == 2 * (row % 128) + row // 128, 1.0, 0.0).astype(jnp.bfloat16)
    merge = jnp.where(row == 2 * (lane % 128) + lane // 128, 1.0, 0.0).astype(jnp.bfloat16)

    feat[64] = jnp.zeros((T, 256), jnp.bfloat16)
    tab[pl.ds(8192, 8)] = jnp.zeros((8, 2, 128), jnp.bfloat16)
    feat_in.wait()

    def build(i, carry):
        s = pl.ds(pl.multiple_of(i * T, T), T)
        rows = feat[i]
        both = jnp.concatenate([rows[:, :128], rows[:, 128:]], axis=0)
        mixed = jnp.dot(merge, both, preferred_element_type=jnp.float32).astype(jnp.bfloat16)
        tab[s] = mixed.reshape(T, 2, 128)
        return carry

    lax.fori_loop(0, 64, build, 0)
    w_in.wait()
    b_in.wait()
    pl.semaphore_wait(barrier, len(peers))

    def gather(dest, r, at):
        base = dest * 512 + r * HALF

        def rows(k, carry):
            for u in range(UNROLL):
                j = k * UNROLL + u
                stage[j] = tab[sidx[base + j]]
            return carry

        lax.fori_loop(0, HALF // UNROLL, rows, 0)
        for h in range(HALF // T):
            both = stage[pl.ds(h * T, T)].reshape(2 * T, 128)
            parts = jnp.dot(split, both, preferred_element_type=jnp.float32).astype(jnp.bfloat16)
            send[at + h, :, 0:128] = parts[:T]
            send[at + h, :, 128:256] = parts[T:]

    def mid_of(i):
        r = i % 2
        j = i // 2
        return r, 1 + j // 3, 1 + j % 3

    def mid_copy(i):
        r, du, dv = mid_of(i)
        ty, tx = place(r, du, 0)
        s = pl.ds(i * 4, 4)
        return remote(
            send.at[s], mid.at[s], mid_send.at[i], mid_recv.at[i], dom_of(ty, tx, c), z
        )

    def mid_step(i, carry):
        r, du, dv = mid_of(i)
        ty, tx = place(r, du, dv)
        for cc in range(2):
            gather(dom_of(ty, tx, (c + cc) % 2), r, i * 4 + cc * 2)
        mid_copy(i).start()
        return carry

    lax.fori_loop(0, 18, mid_step, 0)

    def dir_of(i):
        r = i % 2
        j = i // 2
        g = j // 6
        k = 1 + (j % 6) // 2
        cc = jnp.where(g == 2, 1, j % 2)
        du = jnp.where(g == 0, k, 0)
        dv = jnp.where(g == 1, k, 0)
        ty, tx = place(r, du, dv)
        return r, dom_of(ty, tx, (c + cc) % 2)

    def fin_slot(src, r):
        return pl.ds(src * 4 + r * 2, 2)

    def dir_copy(i):
        r, dest = dir_of(i)
        s = pl.ds(72 + i * 2, 2)
        return remote(
            send.at[s], recv.at[fin_slot(d, r)], dir_send.at[i], fin_recv.at[r * 32 + d], dest, z
        )

    def dir_step(i, carry):
        r, dest = dir_of(i)
        gather(dest, r, 72 + i * 2)
        dir_copy(i).start()
        return carry

    lax.fori_loop(0, 26, dir_step, 0)

    def w_copies(k):
        dst = (z + k) % 4
        return (
            remote(wbuf.at[z], wbuf.at[z], w_send.at[k - 1], w_recv.at[z], d, dst),
            remote(bbuf.at[z], bbuf.at[z], b_send.at[k - 1], b_recv.at[z], d, dst),
        )

    for k in range(1, 4):
        for cp in w_copies(k):
            cp.start()

    def fwd_copy(i, cc):
        r, du, dv = mid_of(i)
        ty, tx = place(r, 0, dv)
        sy, sx = place(r, 4 - du, 0)
        s = pl.ds(i * 4 + cc * 2, 2)
        src = dom_of(sy, sx, c)
        return remote(
            mid.at[s], recv.at[fin_slot(src, r)], fwd_send.at[i * 2 + cc],
            fin_recv.at[r * 32 + src], dom_of(ty, tx, (c + cc) % 2), z,
        )

    def fwd_step(i, carry):
        mid_copy(i).wait_recv()
        for cc in range(2):
            fwd_copy(i, cc).start()
        return carry

    lax.fori_loop(0, 18, fwd_step, 0)

    def tile_sum(slot, tt, idx, base, buf):
        total = None
        for k in (0, 2):
            lhs = jnp.concatenate([abuf[slot, tt, k], abuf[slot, tt, k + 1]], axis=1)
            rhs = jnp.concatenate(
                [buf[idx[base + k]], buf[idx[base + k + 1]]], axis=0
            )
            p = jnp.dot(lhs, rhs, preferred_element_type=jnp.float32)
            total = p if total is None else total + p
        return total

    def local_step(s, carry):
        slot = s % SLOTS
        a_chunk(lval, s, slot).wait()
        for tt in range(2):
            t = s * 2 + tt
            acc[pl.ds(pl.multiple_of(t * T, T), T), :] = tile_sum(slot, tt, lidx, t * 4, feat)

        @pl.when(s + SLOTS < 32)
        def _():
            a_chunk(lval, s + SLOTS, slot).start()

        return carry

    lax.fori_loop(0, 32, local_step, 0)

    def halo_chunk(s):
        q, o = s // 4, s % 4
        plane = (z + jnp.where(o == 0, ZORD[0], jnp.where(o == 1, ZORD[1], jnp.where(o == 2, ZORD[2], 0)))) % 4
        return q, o, plane

    def halo_vals(s, slot):
        q, o, plane = halo_chunk(s)
        return a_chunk(hval, plane * 8 + q, slot)

    for s in range(SLOTS):
        halo_vals(s, s).start()

    recv[pl.ds(d * 4, 4)] = jnp.zeros((4, T, 256), jnp.bfloat16)

    def fin_wait(src, r):
        remote(
            send.at[pl.ds(0, 2)], recv.at[fin_slot(src, r)], dir_send.at[0],
            fin_recv.at[r * 32 + src], d, z,
        ).wait_recv()

    def arrive(k, carry):
        src = (d + k) % 32
        for r in range(2):
            fin_wait(src, r)
        return carry

    lax.fori_loop(1, 32, arrive, 0)

    def z_copy(q, o, plane):
        s = pl.ds(pl.multiple_of(plane * 2048 + q * CH, CH), CH)
        return remote(
            spread.at[s], zrecv.at[z, pl.ds(pl.multiple_of(q * CH, CH), CH)],
            z_send.at[q * 3 + o], z_recv.at[q * 4 + z], d, plane,
        )

    def halo_step(s, carry):
        slot = s % SLOTS
        q, o, plane = halo_chunk(s)
        halo_vals(s, slot).wait()
        for tt in range(2):
            t = (plane * 8 + q) * 2 + tt
            rows = pl.ds(pl.multiple_of(t * T, T), T)
            total = acc[rows, :] + tile_sum(slot, tt, hidx, t * 4, recv)
            spread[rows, :] = total.astype(jnp.bfloat16)

        @pl.when(s + SLOTS < 32)
        def _():
            halo_vals(s + SLOTS, slot).start()

        @pl.when(o < 3)
        def _():
            z_copy(q, o, plane).start()

        return carry

    lax.fori_loop(0, 32, halo_step, 0)

    for k in range(1, 4):
        src = (z + k) % 4
        remote(wbuf.at[src], wbuf.at[src], w_send.at[0], w_recv.at[src], d, src).wait_recv()
        remote(bbuf.at[src], bbuf.at[src], b_send.at[0], b_recv.at[src], d, src).wait_recv()

    part[...] = jnp.zeros_like(part)

    def o_rows(plane, q):
        return pl.ds(pl.multiple_of(plane * 2048 + q * CH, CH), CH)

    def n_rows(q):
        return pl.ds(pl.multiple_of(q * CH, CH), CH)

    def o_copy(q, k):
        dst = (z + k) % 4
        return remote(
            nbuf.at[dst, n_rows(q)], out.at[o_rows(z, q)],
            o_send.at[q * 3 + k - 1], o_recv.at[q * 4 + z], d, dst,
        )

    def own_copy(q):
        return pltpu.make_async_copy(nbuf.at[z, n_rows(q)], out.at[o_rows(z, q)], own_sem.at[q])

    def z_wait(q, src):
        remote(
            spread.at[pl.ds(0, CH)], zrecv.at[src, n_rows(q)], z_send.at[0],
            z_recv.at[q * 4 + src], d, src,
        ).wait_recv()

    def mix_step(q, carry):
        zrecv[z, n_rows(q), :] = spread[o_rows(z, q), :]
        for k in range(1, 4):
            z_wait(q, (z + k) % 4)
        lhs = [zrecv[s, n_rows(q), :] for s in range(4)]
        acts = []
        power = None
        for b in range(4):
            total = None
            for s in range(4):
                p = jnp.dot(
                    lhs[s], wbuf[b, pl.ds(s * 256, 256), :], preferred_element_type=jnp.float32
                )
                total = p if total is None else total + p
            act = jnp.maximum(total + bbuf[b, 0:1, :].astype(jnp.float32), 0.0)
            acts.append(act)
            sq = jnp.sum(act * act, axis=1, keepdims=True)
            power = sq if power is None else power + sq
        scale = lax.rsqrt(power * (1.0 / 1024.0) + epsilon)
        for b in range(4):
            scaled = acts[b] * scale
            part[b, 0:1, :] += jnp.sum(scaled, axis=0, keepdims=True)
            part[b, 1:2, :] += jnp.sum(scaled * scaled, axis=0, keepdims=True)
            nbuf[b, n_rows(q), :] = scaled.astype(jnp.bfloat16)
        for k in (2, 1, 3):
            o_copy(q, k).start()
        own_copy(q).start()
        return carry

    lax.fori_loop(0, 8, mix_step, 0)

    zst[z] = part[z]
    for k in range(1, 4):
        dst = (z + k) % 4
        remote(part.at[dst], zst.at[z], sz_send.at[k - 1], sz_recv.at[z], d, dst).start()
    for k in range(1, 4):
        src = (z + k) % 4
        remote(part.at[src], zst.at[src], sz_send.at[0], sz_recv.at[src], d, src).wait_recv()
    xst[x] = zst[0] + zst[1] + zst[2] + zst[3]
    for k in range(1, 4):
        to = dom_of(y, (x + k) % 4, c)
        remote(xst.at[x], xst.at[x], sx_send.at[k - 1], sx_recv.at[x], to, z).start()
    for k in range(1, 4):
        src = (x + k) % 4
        remote(xst.at[src], xst.at[src], sx_send.at[0], sx_recv.at[src], d, z).wait_recv()
    yst[y] = xst[0] + xst[1] + xst[2] + xst[3]
    for k in range(1, 4):
        to = dom_of((y + k) % 4, x, c)
        remote(yst.at[y], yst.at[y], sy_send.at[k - 1], sy_recv.at[y], to, z).start()
    for k in range(1, 4):
        src = (y + k) % 4
        remote(yst.at[src], yst.at[src], sy_send.at[0], sy_recv.at[src], d, z).wait_recv()
    cst[c] = yst[0] + yst[1] + yst[2] + yst[3]
    other = dom_of(y, x, 1 - c)
    remote(cst.at[c], cst.at[c], sc_send.at[0], sc_recv.at[c], other, z).start()
    remote(cst.at[1 - c], cst.at[1 - c], sc_send.at[0], sc_recv.at[1 - c], other, z).wait_recv()
    sums = (cst[0] + cst[1]) * (1.0 / 262144.0)
    mean = sums[0:1, :]
    stats[0:1, :] = mean
    stats[1:2, :] = sums[1:2, :] - mean * mean

    def mid_done(i, carry):
        mid_copy(i).wait_send()
        for cc in range(2):
            fwd_copy(i, cc).wait_send()
        return carry

    lax.fori_loop(0, 18, mid_done, 0)

    def dir_done(i, carry):
        dir_copy(i).wait_send()
        return carry

    lax.fori_loop(0, 26, dir_done, 0)
    for k in range(1, 4):
        for cp in w_copies(k):
            cp.wait_send()
        dst = (z + k) % 4
        remote(part.at[dst], zst.at[z], sz_send.at[k - 1], sz_recv.at[z], d, dst).wait_send()
        to = dom_of(y, (x + k) % 4, c)
        remote(xst.at[x], xst.at[x], sx_send.at[k - 1], sx_recv.at[x], to, z).wait_send()
        to = dom_of((y + k) % 4, x, c)
        remote(yst.at[y], yst.at[y], sy_send.at[k - 1], sy_recv.at[y], to, z).wait_send()
    remote(cst.at[c], cst.at[c], sc_send.at[0], sc_recv.at[c], other, z).wait_send()

    def z_done(s, carry):
        q, o = s // 3, s % 3
        _, _, plane = halo_chunk(q * 4 + o)
        z_copy(q, o, plane).wait_send()
        return carry

    lax.fori_loop(0, 24, z_done, 0)

    def o_done(q, carry):
        own_copy(q).wait()
        for k in range(1, 4):
            o_copy(q, k).wait_send()
            src = (z + k) % 4
            remote(
                nbuf.at[0, n_rows(q)], out.at[o_rows(src, q)], o_send.at[0],
                o_recv.at[q * 4 + src], d, src,
            ).wait_recv()
        return carry

    lax.fori_loop(0, 8, o_done, 0)


def on_device(
    features, weight, out_bias, local_index, local_count, local_vals,
    halo_index, halo_count, halo_vals, send_rows, send_count,
):
    d = lax.axis_index("dom")
    slot = jnp.arange(512)[None, :]
    sidx = jnp.where(slot < send_count[0][:, None], send_rows[0], 8192).reshape(-1)
    four = jnp.arange(4)[None, :]
    lidx = jnp.where(four < local_count[0][:, None], local_index[0], 64).reshape(-1)
    hidx = jnp.where(four < halo_count[0][:, None], halo_index[0], d * 4).reshape(-1)
    bias = jnp.broadcast_to(out_bias[None, :], (16, 256))
    smem = pl.BlockSpec(memory_space=pltpu.SMEM)
    hbm = pl.BlockSpec(memory_space=pl.ANY)
    bf16, f32 = jnp.bfloat16, jnp.float32
    V = pltpu.VMEM
    dma = pltpu.SemaphoreType.DMA
    out, stats = pl.pallas_call(
        layer,
        out_shape=(
            jax.ShapeDtypeStruct((8192, 256), bf16),
            jax.ShapeDtypeStruct((2, 256), f32),
        ),
        in_specs=[smem, smem, smem, hbm, hbm, hbm, hbm, hbm],
        out_specs=(hbm, pl.BlockSpec(memory_space=V)),
        scratch_shapes=[
            V((65, T, 256), bf16),
            V((8192 + 8, 2, 128), bf16),
            V((HALF, 2, 128), bf16),
            V((72 + 26 * 2, T, 256), bf16),
            V((72, T, 256), bf16),
            V((128, T, 256), bf16),
            V((8192, 256), f32),
            V((SLOTS, 2, 4, 128, 128), bf16),
            V((8192, 256), bf16),
            V((4, 2048, 256), bf16),
            V((4, 1024, 256), bf16),
            V((4, 16, 256), bf16),
            V((4, 2048, 256), bf16),
            V((4, 8, 256), f32),
            V((4, 8, 256), f32),
            V((4, 8, 256), f32),
            V((4, 8, 256), f32),
            V((2, 8, 256), f32),
            dma((3,)), dma((SLOTS,)), dma((3,)), dma((4,)), dma((3,)), dma((4,)),
            dma((18,)), dma((18,)), dma((26,)), dma((36,)), dma((64,)),
            dma((24,)), dma((32,)), dma((24,)), dma((32,)), dma((8,)),
            dma((3,)), dma((4,)), dma((3,)), dma((4,)), dma((3,)), dma((4,)), dma((1,)), dma((2,)),
        ],
        compiler_params=pltpu.CompilerParams(
            collective_id=0, has_side_effects=True, vmem_limit_bytes=67043328
        ),
        name="layer",
    )(sidx, lidx, hidx, features.reshape(64, T, 256), weight, bias, local_vals[0], halo_vals[0])
    return out, stats


def solution(mesh):
    in_specs = (
        P("dom", "col"), P(None, "col"), P("col"),
        P("dom", None, None), P("dom", None), P("dom", None, None, None, None),
        P("dom", None, None), P("dom", None), P("dom", None, None, None, None),
        P("dom", None, None), P("dom", None),
    )
    return jax.shard_map(
        on_device, mesh=mesh, in_specs=in_specs,
        out_specs=(P("dom", "col"), P(None, "col")), check_vma=False,
    )
```

time: 366 us -> 244 us (0.67)
  Pallas kernels: 0 us -> 226 us
  waiting for transfers between devices: 130 us -> 0 us
  local copies, waits for them, and re-layouts: 109 us -> 9.16 us
  blocking collectives: 53.2 us -> 0 us
  matrix products: 34.7 us -> 0 us
  starting transfers between devices: 23 us -> 0 us
  other arithmetic: 14.1 us -> 3.43 us
    pallas_call x0 -> x1, Pallas kernels: none -> 226 us  [on_device(): pl.pallas_call(layer, out_shape=(jax.ShapeDtypeStruct((8192, 256), bf16),...]
    all_to_all x4 -> x0, waiting for transfers between devices: 130 us -> none  [the longest x1 86.1 us: on_device(): lax.all_to_all(outgoing, DOM, split_axis=0, concat_axis=0, tiled=True)]
    gather x3 -> x0, local copies, waits for them, and re-layouts: 88.7 us -> none  [the longest x1 63.5 us: on_device(): chosen = features[send_rows[0]]]
    psum x4 -> x0, blocking collectives: 53.2 us -> none  [one_axis_at_a_time(): return functools.reduce(lax.psum, axes, value)]
    dot_general x3 -> x0, matrix products: 34.7 us -> none  [the longest x2 27.7 us: tile_sum(): jnp.einsum('tkij,tkjc->tic', masked, gathered, preferred_element_type=jnp...]
    all_to_all x4 -> x0, starting transfers between devices: 23 us -> none  [the longest x1 7.76 us: on_device(): lax.all_to_all(outgoing, DOM, split_axis=0, concat_axis=0, tiled=True)]
    all_to_all x2 -> x0, local copies, waits for them, and re-layouts: 9.12 us -> none  [the longest x1 6.18 us: on_device(): lax.all_to_all(scaled.astype(jnp.bfloat16), 'col', split_axis=1, concat_a...]
    select_n x3 -> x2, other arithmetic: 8.07 us -> 1.23 us  [the longest x1 0.64 us: on_device(): jnp.where(slot < send_count[0][:, None], send_rows[0], 8192).reshape(-1)]
  transfers between devices with their start and end apart: 4 -> 0, of which waited for: 2 -> 0; matrix products, arithmetic and copies ran while one was open for 18% -> 0% of each run, Pallas kernels for 0% -> 0%
where the time goes in v1:
time: 244 us; the launch traced here: 240 us
  Pallas kernels  226 us (93%)
  local copies, waits for them, and re-layouts  9.16 us (4%)
  other arithmetic  3.43 us (1%)
    pallas_call x1, Pallas kernels, on_device(): pl.pallas_call(layer, out_shape=(jax.ShapeDtypeStruct((8192, 256), bf16),...  226 us
    unnamed x8, local copies, waits for them, and re-layouts  7.48 us

profile of v1, /device:TPU:6, one launch (start us, length us, event | category | flops | bytes accessed | tf_op | source)
XLA Modules:
  0.0 239.7 jit_solution(18035111469511079205)
XLA Ops:
  0.6 1.3 broadcast_in_dim.23.bias_hbm
  1.9 0.7 iota_compare_fusion.2
  2.6 0.1 lt.66
  2.7 0.7 iota_compare_fusion.1
  3.5 0.1 lt.71
  3.6 0.7 fusion
  4.4 0.8 copy.13
  5.1 0.1 squeeze.16
  5.2 0.8 copy.14
  6.0 0.1 squeeze.17
  6.1 0.6 broadcast_select_fusion.1
  6.7 0.9 copy.16
  7.6 0.6 broadcast_select_fusion.sidx
  8.2 226.5 %layer.1 = (bf16[8192,256]{1,0:T(8,128)(2,1)}, f32[2,256]{1,0:T(2,128)}) custom-call(s32[16384]{0:T(1024)} %broadcast_select_fusion.sidx, s32[256]{0:T(256)} %get-tuple-element.3.lidx, s32[256]{0:T(256)} %get-tuple-element.2.hidx, bf16[64,128,256]{2,1,0:T(8,128)(2,1)} %bitcast.13, bf16[1024,256]{1,0:T(8,128)(2,1)} %w_hbm.1, ...), custom_call_target="tpu_custom_call" | custom-call | tf_op jit(solution)/shard_map/layer/pallas_call | solution.py:433
  234.7 0.0 copy-start
  234.7 4.5 %copy.19 = bf16[8192,256]{1,0:T(8,128)(2,1)} copy(bf16[8192,256]{1,0:T(8,128)(2,1)} %get-tuple-element.6) | data formatting | bytes 8388608
  239.2 0.0 copy-done
  239.2 0.6 copy.20
  (1 shorter events, 0.0 us)
Async XLA Ops:
  234.7 4.5 %copy-start = (f32[2,256]{1,0:T(2,128)S(1)}, f32[2,256]{1,0:T(2,128)}, u32[]{:S(2)}) copy-start(f32[2,256]{1,0:T(2,128)} %get-tuple-element.7) | copy-start | bytes 6148

commit v2 on v1

--- a/solution.py
+++ b/solution.py
@@ -12,7 +12,7 @@
 
 T = 128
 HALF = 256
-UNROLL = 32
+G = 64
 ZORD = (2, 1, 3)
 CH = 256
 SLOTS = 4
@@ -23,7 +23,7 @@
 
 
 def layer(
-    sidx, lidx, hidx, feat_hbm, w_hbm, bias_hbm, lval, hval,
+    sidx, scnt, lidx, lcnt, hidx, hcnt, feat_hbm, w_hbm, bias_hbm, lval, hval,
     out, stats,
     feat, tab, stage, send, mid, recv, acc, abuf, spread, zrecv, wbuf, bbuf, nbuf,
     part, zst, xst, yst, cst,
@@ -77,46 +77,49 @@
 
     row = lax.broadcasted_iota(jnp.int32, (256, 256), 0)
     lane = lax.broadcasted_iota(jnp.int32, (256, 256), 1)
-    split = jnp.where(lane == 2 * (row % 128) + row // 128, 1.0, 0.0).astype(jnp.bfloat16)
+    srow = lax.broadcasted_iota(jnp.int32, (2 * G, 2 * G), 0)
+    slane = lax.broadcasted_iota(jnp.int32, (2 * G, 2 * G), 1)
+    split = jnp.where(slane == 2 * (srow % G) + srow // G, 1.0, 0.0).astype(jnp.bfloat16)
     merge = jnp.where(row == 2 * (lane % 128) + lane // 128, 1.0, 0.0).astype(jnp.bfloat16)
 
     feat[64] = jnp.zeros((T, 256), jnp.bfloat16)
-    tab[pl.ds(8192, 8)] = jnp.zeros((8, 2, 128), jnp.bfloat16)
     feat_in.wait()
 
     def build(i, carry):
-        s = pl.ds(pl.multiple_of(i * T, T), T)
-        rows = feat[i]
-        both = jnp.concatenate([rows[:, :128], rows[:, 128:]], axis=0)
-        mixed = jnp.dot(merge, both, preferred_element_type=jnp.float32).astype(jnp.bfloat16)
-        tab[s] = mixed.reshape(T, 2, 128)
-        return carry
-
-    lax.fori_loop(0, 64, build, 0)
+        mixed = []
+        for u in range(8):
+            rows = feat[i * 8 + u]
+            both = jnp.concatenate([rows[:, :128], rows[:, 128:]], axis=0)
+            mixed.append(jnp.dot(merge, both, preferred_element_type=jnp.float32).astype(jnp.bfloat16))
+        for u in range(8):
+            s = pl.ds(pl.multiple_of(i * 1024 + u * T, T), T)
+            tab[s] = mixed[u].reshape(T, 2, 128)
+        return carry
+
+    lax.fori_loop(0, 8, build, 0)
     w_in.wait()
     b_in.wait()
     pl.semaphore_wait(barrier, len(peers))
 
+    row_id = lax.broadcasted_iota(jnp.int32, (G, 128), 0)
+
     def gather(dest, r, at):
-        base = dest * 512 + r * HALF
-
-        def rows(k, carry):
-            for u in range(UNROLL):
-                j = k * UNROLL + u
-                stage[j] = tab[sidx[base + j]]
-            return carry
-
-        lax.fori_loop(0, HALF // UNROLL, rows, 0)
-        for h in range(HALF // T):
-            both = stage[pl.ds(h * T, T)].reshape(2 * T, 128)
-            parts = jnp.dot(split, both, preferred_element_type=jnp.float32).astype(jnp.bfloat16)
-            send[at + h, :, 0:128] = parts[:T]
-            send[at + h, :, 128:256] = parts[T:]
+        used = scnt[0, dest] - r * HALF
+        for g in range(HALF // G):
+            for u in range(G):
+                stage[g * G + u] = tab[sidx[dest, r * HALF + g * G + u]]
+            both = stage[pl.ds(g * G, G)].reshape(2 * G, 128)
+            parts = jnp.dot(split, both, preferred_element_type=jnp.float32)
+            keep = row_id < used - g * G
+            rows = pl.ds(g * G % T, G)
+            for h in range(2):
+                half = jnp.where(keep, parts[h * G : (h + 1) * G], 0.0)
+                send[at + g * G // T, rows, h * 128 : (h + 1) * 128] = half.astype(jnp.bfloat16)
 
     def mid_of(i):
         r = i % 2
         j = i // 2
-        return r, 1 + j // 3, 1 + j % 3
+        return r, 1 + (j * 2) % 3, 1 + j // 3
 
     def mid_copy(i):
         r, du, dv = mid_of(i)
@@ -157,25 +160,6 @@
             send.at[s], recv.at[fin_slot(d, r)], dir_send.at[i], fin_recv.at[r * 32 + d], dest, z
         )
 
-    def dir_step(i, carry):
-        r, dest = dir_of(i)
-        gather(dest, r, 72 + i * 2)
-        dir_copy(i).start()
-        return carry
-
-    lax.fori_loop(0, 26, dir_step, 0)
-
-    def w_copies(k):
-        dst = (z + k) % 4
-        return (
-            remote(wbuf.at[z], wbuf.at[z], w_send.at[k - 1], w_recv.at[z], d, dst),
-            remote(bbuf.at[z], bbuf.at[z], b_send.at[k - 1], b_recv.at[z], d, dst),
-        )
-
-    for k in range(1, 4):
-        for cp in w_copies(k):
-            cp.start()
-
     def fwd_copy(i, cc):
         r, du, dv = mid_of(i)
         ty, tx = place(r, 0, dv)
@@ -187,20 +171,42 @@
             fin_recv.at[r * 32 + src], dom_of(ty, tx, (c + cc) % 2), z,
         )
 
-    def fwd_step(i, carry):
+    def fwd_step(i):
         mid_copy(i).wait_recv()
         for cc in range(2):
             fwd_copy(i, cc).start()
-        return carry
-
-    lax.fori_loop(0, 18, fwd_step, 0)
-
-    def tile_sum(slot, tt, idx, base, buf):
+
+    def dir_step(i, carry):
+        r, dest = dir_of(i)
+        gather(dest, r, 72 + i * 2)
+        dir_copy(i).start()
+
+        @pl.when(i < 18)
+        def _():
+            fwd_step(i)
+
+        return carry
+
+    lax.fori_loop(0, 26, dir_step, 0)
+
+    def w_copies(k):
+        dst = (z + k) % 4
+        return (
+            remote(wbuf.at[z], wbuf.at[z], w_send.at[k - 1], w_recv.at[z], d, dst),
+            remote(bbuf.at[z], bbuf.at[z], b_send.at[k - 1], b_recv.at[z], d, dst),
+        )
+
+    for k in range(1, 4):
+        for cp in w_copies(k):
+            cp.start()
+
+    def tile_sum(slot, tt, idx, cnt, zero, t, buf):
         total = None
+        at = [jnp.where(k < cnt[0, t], idx[k, t], zero) for k in range(4)]
         for k in (0, 2):
             lhs = jnp.concatenate([abuf[slot, tt, k], abuf[slot, tt, k + 1]], axis=1)
             rhs = jnp.concatenate(
-                [buf[idx[base + k]], buf[idx[base + k + 1]]], axis=0
+                [buf[at[k]], buf[at[k + 1]]], axis=0
             )
             p = jnp.dot(lhs, rhs, preferred_element_type=jnp.float32)
             total = p if total is None else total + p
@@ -211,7 +217,7 @@
         a_chunk(lval, s, slot).wait()
         for tt in range(2):
             t = s * 2 + tt
-            acc[pl.ds(pl.multiple_of(t * T, T), T), :] = tile_sum(slot, tt, lidx, t * 4, feat)
+            acc[pl.ds(pl.multiple_of(t * T, T), T), :] = tile_sum(slot, tt, lidx, lcnt, 64, t, feat)
 
         @pl.when(s + SLOTS < 32)
         def _():
@@ -263,7 +269,7 @@
         for tt in range(2):
             t = (plane * 8 + q) * 2 + tt
             rows = pl.ds(pl.multiple_of(t * T, T), T)
-            total = acc[rows, :] + tile_sum(slot, tt, hidx, t * 4, recv)
+            total = acc[rows, :] + tile_sum(slot, tt, hidx, hcnt, d * 4, t, recv)
             spread[rows, :] = total.astype(jnp.bfloat16)
 
         @pl.when(s + SLOTS < 32)
@@ -321,7 +327,7 @@
                     lhs[s], wbuf[b, pl.ds(s * 256, 256), :], preferred_element_type=jnp.float32
                 )
                 total = p if total is None else total + p
-            act = jnp.maximum(total + bbuf[b, 0:1, :].astype(jnp.float32), 0.0)
+            act = jnp.maximum(total + bbuf[b].astype(jnp.float32), 0.0)
             acts.append(act)
             sq = jnp.sum(act * act, axis=1, keepdims=True)
             power = sq if power is None else power + sq
@@ -338,35 +344,41 @@
 
     lax.fori_loop(0, 8, mix_step, 0)
 
-    zst[z] = part[z]
-    for k in range(1, 4):
+    def x_sum(k):
+        to = dom_of(y, (x + k) % 4, c)
+        return remote(xst.at[x], xst.at[x], sx_send.at[k - 1], sx_recv.at[x], to, z)
+
+    def y_sum(k):
+        to = dom_of((y + k) % 4, x, c)
+        return remote(yst.at[y], yst.at[y], sy_send.at[k - 1], sy_recv.at[y], to, z)
+
+    def c_sum():
+        to = dom_of(y, x, 1 - c)
+        return remote(cst.at[c], cst.at[c], sc_send.at[0], sc_recv.at[c], to, z)
+
+    def z_sum(k):
         dst = (z + k) % 4
-        remote(part.at[dst], zst.at[z], sz_send.at[k - 1], sz_recv.at[z], d, dst).start()
-    for k in range(1, 4):
-        src = (z + k) % 4
-        remote(part.at[src], zst.at[src], sz_send.at[0], sz_recv.at[src], d, src).wait_recv()
-    xst[x] = zst[0] + zst[1] + zst[2] + zst[3]
-    for k in range(1, 4):
-        to = dom_of(y, (x + k) % 4, c)
-        remote(xst.at[x], xst.at[x], sx_send.at[k - 1], sx_recv.at[x], to, z).start()
+        return remote(part.at[dst], zst.at[z], sz_send.at[k - 1], sz_recv.at[z], d, dst)
+
+    xst[x] = part[...]
+    for k in range(1, 4):
+        x_sum(k).start()
     for k in range(1, 4):
         src = (x + k) % 4
         remote(xst.at[src], xst.at[src], sx_send.at[0], sx_recv.at[src], d, z).wait_recv()
     yst[y] = xst[0] + xst[1] + xst[2] + xst[3]
     for k in range(1, 4):
-        to = dom_of((y + k) % 4, x, c)
-        remote(yst.at[y], yst.at[y], sy_send.at[k - 1], sy_recv.at[y], to, z).start()
+        y_sum(k).start()
     for k in range(1, 4):
         src = (y + k) % 4
         remote(yst.at[src], yst.at[src], sy_send.at[0], sy_recv.at[src], d, z).wait_recv()
     cst[c] = yst[0] + yst[1] + yst[2] + yst[3]
-    other = dom_of(y, x, 1 - c)
-    remote(cst.at[c], cst.at[c], sc_send.at[0], sc_recv.at[c], other, z).start()
-    remote(cst.at[1 - c], cst.at[1 - c], sc_send.at[0], sc_recv.at[1 - c], other, z).wait_recv()
-    sums = (cst[0] + cst[1]) * (1.0 / 262144.0)
-    mean = sums[0:1, :]
-    stats[0:1, :] = mean
-    stats[1:2, :] = sums[1:2, :] - mean * mean
+    c_sum().start()
+    remote(cst.at[1 - c], cst.at[1 - c], sc_send.at[0], sc_recv.at[1 - c], d, z).wait_recv()
+    part[...] = cst[0] + cst[1]
+    zst[z] = part[z]
+    for k in range(1, 4):
+        z_sum(k).start()
 
     def mid_done(i, carry):
         mid_copy(i).wait_send()
@@ -384,13 +396,9 @@
     for k in range(1, 4):
         for cp in w_copies(k):
             cp.wait_send()
-        dst = (z + k) % 4
-        remote(part.at[dst], zst.at[z], sz_send.at[k - 1], sz_recv.at[z], d, dst).wait_send()
-        to = dom_of(y, (x + k) % 4, c)
-        remote(xst.at[x], xst.at[x], sx_send.at[k - 1], sx_recv.at[x], to, z).wait_send()
-        to = dom_of((y + k) % 4, x, c)
-        remote(yst.at[y], yst.at[y], sy_send.at[k - 1], sy_recv.at[y], to, z).wait_send()
-    remote(cst.at[c], cst.at[c], sc_send.at[0], sc_recv.at[c], other, z).wait_send()
+        x_sum(k).wait_send()
+        y_sum(k).wait_send()
+    c_sum().wait_send()
 
     def z_done(s, carry):
         q, o = s // 3, s % 3
@@ -413,18 +421,20 @@
 
     lax.fori_loop(0, 8, o_done, 0)
 
+    for k in range(1, 4):
+        src = (z + k) % 4
+        remote(part.at[src], zst.at[src], sz_send.at[0], sz_recv.at[src], d, src).wait_recv()
+        z_sum(k).wait_send()
+    sums = (zst[0] + zst[1] + zst[2] + zst[3]) * (1.0 / 262144.0)
+    mean = sums[0:1, :]
+    stats[0:1, :] = mean
+    stats[1:2, :] = sums[1:2, :] - mean * mean
+
 
 def on_device(
     features, weight, out_bias, local_index, local_count, local_vals,
     halo_index, halo_count, halo_vals, send_rows, send_count,
 ):
-    d = lax.axis_index("dom")
-    slot = jnp.arange(512)[None, :]
-    sidx = jnp.where(slot < send_count[0][:, None], send_rows[0], 8192).reshape(-1)
-    four = jnp.arange(4)[None, :]
-    lidx = jnp.where(four < local_count[0][:, None], local_index[0], 64).reshape(-1)
-    hidx = jnp.where(four < halo_count[0][:, None], halo_index[0], d * 4).reshape(-1)
-    bias = jnp.broadcast_to(out_bias[None, :], (16, 256))
     smem = pl.BlockSpec(memory_space=pltpu.SMEM)
     hbm = pl.BlockSpec(memory_space=pl.ANY)
     bf16, f32 = jnp.bfloat16, jnp.float32
@@ -436,11 +446,11 @@
             jax.ShapeDtypeStruct((8192, 256), bf16),
             jax.ShapeDtypeStruct((2, 256), f32),
         ),
-        in_specs=[smem, smem, smem, hbm, hbm, hbm, hbm, hbm],
+        in_specs=[smem] * 6 + [hbm, hbm, hbm, hbm, hbm],
         out_specs=(hbm, pl.BlockSpec(memory_space=V)),
         scratch_shapes=[
             V((65, T, 256), bf16),
-            V((8192 + 8, 2, 128), bf16),
+            V((8192, 2, 128), bf16),
             V((HALF, 2, 128), bf16),
             V((72 + 26 * 2, T, 256), bf16),
             V((72, T, 256), bf16),
@@ -450,13 +460,13 @@
             V((8192, 256), bf16),
             V((4, 2048, 256), bf16),
             V((4, 1024, 256), bf16),
-            V((4, 16, 256), bf16),
+            V((4, 1, 256), bf16),
             V((4, 2048, 256), bf16),
-            V((4, 8, 256), f32),
-            V((4, 8, 256), f32),
-            V((4, 8, 256), f32),
-            V((4, 8, 256), f32),
-            V((2, 8, 256), f32),
+            V((4, 2, 256), f32),
+            V((4, 2, 256), f32),
+            V((4, 4, 2, 256), f32),
+            V((4, 4, 2, 256), f32),
+            V((2, 4, 2, 256), f32),
             dma((3,)), dma((SLOTS,)), dma((3,)), dma((4,)), dma((3,)), dma((4,)),
             dma((18,)), dma((18,)), dma((26,)), dma((36,)), dma((64,)),
             dma((24,)), dma((32,)), dma((24,)), dma((32,)), dma((8,)),
@@ -466,7 +476,10 @@
             collective_id=0, has_side_effects=True, vmem_limit_bytes=67043328
         ),
         name="layer",
-    )(sidx, lidx, hidx, features.reshape(64, T, 256), weight, bias, local_vals[0], halo_vals[0])
+    )(
+        send_rows[0], send_count, local_index[0].T, local_count, halo_index[0].T, halo_count,
+        features.reshape(64, T, 256), weight, out_bias.reshape(1, 256), local_vals[0], halo_vals[0],
+    )
     return out, stats
 
 

time: 244 us -> 214 us (0.88); the launches traced: 240 us -> 212 us
  Pallas kernels: 226 us -> 205 us
  other arithmetic: 3.43 us -> 0 us
  local copies, waits for them, and re-layouts: 9.16 us -> 6.27 us
    pallas_call x1, Pallas kernels: 226 us -> 205 us  [on_device(): pl.pallas_call(layer, out_shape=(jax.ShapeDtypeStruct((8192, 256), bf16),...]
    unnamed x8 -> x4, local copies, waits for them, and re-layouts: 7.48 us -> 5.05 us
where the time goes in v2:
time: 214 us; the launch traced here: 212 us
  Pallas kernels  205 us (96%)
  local copies, waits for them, and re-layouts  6.27 us (3%)
    pallas_call x1, Pallas kernels, on_device(): pl.pallas_call(layer, out_shape=(jax.ShapeDtypeStruct((8192, 256), bf16),...  205 us
    unnamed x4, local copies, waits for them, and re-layouts  5.05 us

profile of v2, /device:TPU:6, one launch (start us, length us, event | category | flops | bytes accessed | tf_op | source)
XLA Modules:
  0.0 212.3 jit_solution(17268464415429199552)
XLA Ops:
  0.6 1.2 reshape.11.bias_hbm
  1.9 205.4 %layer.1 = (bf16[8192,256]{1,0:T(8,128)(2,1)}, f32[2,256]{1,0:T(2,128)}) custom-call(s32[32,512]{1,0:T(8,128)} %bitcast.13, s32[1,32]{1,0:T(1,128)} %scnt.1, s32[4,64]{1,0:T(4,128)} %bitcast.14, s32[1,64]{1,0:T(1,128)} %lcnt.1, s32[4,64]{1,0:T(4,128)} %bitcast.15, s32[1,64]{1,0:T(1,128)} %hcnt.1, bf16[64,128,256]{2,1,0:T(8,128)(2,1)} %bitcast.12, ...), custom_call_target="tpu_custom_call" | custom-call | tf_op jit(solution)/shard_map/layer/pallas_call | solution.py:443
  207.3 0.0 copy-start
  207.3 4.5 %copy.15 = bf16[8192,256]{1,0:T(8,128)(2,1)} copy(bf16[8192,256]{1,0:T(8,128)(2,1)} %get-tuple-element.4) | data formatting | bytes 8388608
  211.8 0.0 copy-done
  211.8 0.6 copy.16
Async XLA Ops:
  207.3 4.5 %copy-start = (f32[2,256]{1,0:T(2,128)S(1)}, f32[2,256]{1,0:T(2,128)}, u32[]{:S(2)}) copy-start(f32[2,256]{1,0:T(2,128)} %get-tuple-element.5) | copy-start | bytes 6148

commit v3 on v2

v3 whole, which is shorter than its diff:
```python
import jax
import jax.numpy as jnp
from jax import lax
from jax.experimental import pallas as pl
from jax.experimental.pallas import tpu as pltpu
from jax.sharding import PartitionSpec as P

MESH = pl.DeviceIdType.MESH
epsilon = 1e-06

T = 128
HALF = 256
G = 64
ZORD = (2, 1, 3)
SPLIT = 12
SLOTS = 4
N = 128


def dom_of(y, x, c):
    return (y * 4 + x) * 2 + c


def layer(
    sidx, scnt, lidx, lcnt, hidx, hcnt, feat_hbm, w_hbm, bias_hbm, lval, hval,
    out, stats,
    feat, tab, stage, send, mid, mid2, recv, recv2, acc, abuf, zrecv, wbuf, bbuf, nbuf,
    zb, ya, pa, pb, part, s1, s2,
    in_sem, a_sem, w_send, w_recv, wg_send, wg_recv, b_send, b_recv,
    mid_send, mid_recv, mid_recv2, dir_send, fwd_send, fin_recv, fin_recv2,
    z_send, z_recv, z_recv2, n_send, zb_recv, o_recv, pa_send, pa_recv, pb_send, pb_recv,
    s1_send, s1_recv, s2_send, s2_recv,
):
    f32, bf16 = jnp.float32, jnp.bfloat16
    d = lax.axis_index("dom")
    z = lax.axis_index("col")
    y, x, c = d // 8, (d // 2) % 4, d % 2

    def place(r, du, dv):
        dy = jnp.where(r == 0, dv, du)
        dx = jnp.where(r == 0, du, dv)
        return (y + dy) % 4, (x + dx) % 4

    def remote(src, dst, ssem, rsem, dom, col):
        return pltpu.make_async_remote_copy(
            src_ref=src, dst_ref=dst, send_sem=ssem, recv_sem=rsem,
            device_id={"dom": dom, "col": col}, device_id_type=MESH,
        )

    barrier = pltpu.get_barrier_semaphore()
    peers = []
    for k in range(1, 4):
        for cc in range(2):
            peers.append((dom_of(y, (x + k) % 4, cc), z))
            peers.append((dom_of((y + k) % 4, x, cc), z))
        peers.append((d, (z + k) % 4))
    peers.append((dom_of(y, x, 1 - c), z))
    for dom, col in peers:
        pl.semaphore_signal(
            barrier, inc=1, device_id={"dom": dom, "col": col}, device_id_type=MESH
        )

    feat_in = pltpu.make_async_copy(feat_hbm, feat.at[pl.ds(0, 64)], in_sem.at[0])
    feat_in.start()
    w_in = pltpu.make_async_copy(w_hbm, wbuf.at[z], in_sem.at[1])
    w_in.start()
    b_in = pltpu.make_async_copy(bias_hbm, bbuf.at[z], in_sem.at[2])
    b_in.start()

    def a_chunk(vals, chunk, slot):
        return pltpu.make_async_copy(vals.at[pl.ds(chunk * 2, 2)], abuf.at[slot], a_sem.at[slot])

    for s in range(SLOTS):
        a_chunk(lval, s, s).start()

    row = lax.broadcasted_iota(jnp.int32, (256, 256), 0)
    lane = lax.broadcasted_iota(jnp.int32, (256, 256), 1)
    merge = jnp.where(row == 2 * (lane % 128) + lane // 128, 1.0, 0.0).astype(bf16)
    srow = lax.broadcasted_iota(jnp.int32, (2 * G, 2 * G), 0)
    slane = lax.broadcasted_iota(jnp.int32, (2 * G, 2 * G), 1)
    split = jnp.where(slane == 2 * (srow % G) + srow // G, 1.0, 0.0).astype(bf16)
    row_id = lax.broadcasted_iota(jnp.int32, (G, 128), 0)
    lane_id = lax.broadcasted_iota(jnp.int32, (G, 128), 1)

    feat[64] = jnp.zeros((T, 256), bf16)
    zb[64] = jnp.zeros((T, N), bf16)
    feat_in.wait()

    def build(i, carry):
        mixed = []
        for u in range(8):
            rows = feat[i * 8 + u]
            both = jnp.concatenate([rows[:, :128], rows[:, 128:]], axis=0)
            mixed.append(jnp.dot(merge, both, preferred_element_type=f32).astype(bf16))
        for u in range(8):
            tab[pl.ds(pl.multiple_of(i * 1024 + u * T, T), T)] = mixed[u].reshape(T, 2, 128)
        return carry

    lax.fori_loop(0, 8, build, 0)
    w_in.wait()
    b_in.wait()
    pl.semaphore_wait(barrier, len(peers))

    other = dom_of(y, x, 1 - c)

    def w_part(plane, h, core):
        return wbuf.at[plane, pl.ds(core * 512, 512), pl.ds(h * N, N)]

    def w_copy(k, h):
        part = w_part(z, h, c)
        return remote(part, part, w_send.at[h * 3 + k - 1], w_recv.at[h * 4 + z], d, (z + k) % 4)

    def w_give(k, h):
        src = (z + k) % 4
        part = w_part(src, h, c)
        return remote(part, part, wg_send.at[h * 3 + k - 1], wg_recv.at[h * 4 + src], other, z)

    def bias_copy(k):
        return remote(bbuf.at[z], bbuf.at[z], b_send.at[k - 1], b_recv.at[z], d, (z + k) % 4)

    def w_wait(h):
        for k in range(1, 4):
            src = (z + k) % 4
            part = w_part(src, h, c)
            remote(part, part, w_send.at[0], w_recv.at[h * 4 + src], d, src).wait_recv()
            w_give(k, h).start()
        for k in range(1, 4):
            src = (z + k) % 4
            part = w_part(src, h, 1 - c)
            remote(part, part, wg_send.at[0], wg_recv.at[h * 4 + src], d, z).wait_recv()

    for k in range(1, 4):
        w_copy(k, 1).start()

    def z_plane(o):
        far = jnp.where(o == 0, ZORD[0], jnp.where(o == 1, ZORD[1], jnp.where(o == 2, ZORD[2], 0)))
        return (z + far) % 4

    def z_copy(q, o, sems):
        plane = z_plane(o)
        return remote(
            feat.at[pl.ds(plane * 16 + q * 2, 2)], zrecv.at[z, pl.ds(q * 2, 2)],
            z_send.at[q * 3 + o], sems.at[q * 4 + z], d, plane,
        )

    def z_first(s, carry):
        z_copy(s // 3, s % 3, z_recv).start()
        return carry

    lax.fori_loop(0, 24, z_first, 0)

    def gather(dest, r, at, narrow):
        used = scnt[0, dest] - r * HALF
        base = dest * 512 + r * HALF
        for g in range(HALF // G):
            for u in range(G):
                stage[g * G + u] = tab[sidx[base + (g * G + u)]]
            both = stage[pl.ds(g * G, G)].reshape(2 * G, 128)
            parts = jnp.dot(split, both, preferred_element_type=f32)
            keep = row_id < used - g * G
            rows = pl.ds(g * G % T, G)
            if narrow:
                whole = jnp.where(lane_id < 64, parts[:G], pltpu.roll(parts[G:], 64, 1))
                send[at + g * G // T, rows, 0:128] = jnp.where(keep, whole, 0.0).astype(bf16)
            else:
                for h in range(2):
                    half = jnp.where(keep, parts[h * G : (h + 1) * G], 0.0)
                    send[at + g * G // T, rows, h * 128 : (h + 1) * 128] = half.astype(bf16)

    def mid_of(i):
        r = i % 2
        j = i // 2
        return r, 1 + (j * 2) % 3, 1 + j // 3

    def sent(at, n, narrow):
        return send.at[pl.ds(at, n), :, pl.ds(0, 128)] if narrow else send.at[pl.ds(at, n)]

    def mid_copy(i, narrow):
        r, du, dv = mid_of(i)
        ty, tx = place(r, du, 0)
        buf, sems = (mid2, mid_recv2) if narrow else (mid, mid_recv)
        return remote(
            sent(i * 4, 4, narrow), buf.at[pl.ds(i * 4, 4)], mid_send.at[i], sems.at[i],
            dom_of(ty, tx, c), z,
        )

    def mid_step(i, narrow):
        r, du, dv = mid_of(i)
        ty, tx = place(r, du, dv)

        def core(cc, carry):
            gather(dom_of(ty, tx, (c + cc) % 2), r, i * 4 + cc * 2, narrow)
            return carry

        lax.fori_loop(0, 2, core, 0)
        mid_copy(i, narrow).start()

    def dir_of(i):
        r = i % 2
        j = i // 2
        g = j // 6
        k = 1 + (j % 6) // 2
        cc = jnp.where(g == 2, 1, j % 2)
        du = jnp.where(g == 0, k, 0)
        dv = jnp.where(g == 1, k, 0)
        ty, tx = place(r, du, dv)
        return r, dom_of(ty, tx, (c + cc) % 2)

    def fin_at(src, r, narrow):
        buf, sems = (recv2, fin_recv2) if narrow else (recv, fin_recv)
        return buf.at[pl.ds(src * 4 + r * 2, 2)], sems.at[r * 32 + src]

    def dir_copy(i, narrow):
        r, dest = dir_of(i)
        dst, sem = fin_at(d, r, narrow)
        return remote(sent(72 + i * 2, 2, narrow), dst, dir_send.at[i], sem, dest, z)

    def fwd_copy(i, cc, narrow):
        r, du, dv = mid_of(i)
        ty, tx = place(r, 0, dv)
        sy, sx = place(r, 4 - du, 0)
        dst, sem = fin_at(dom_of(sy, sx, c), r, narrow)
        buf = mid2 if narrow else mid
        return remote(
            buf.at[pl.ds(i * 4 + cc * 2, 2)], dst, fwd_send.at[i * 2 + cc], sem,
            dom_of(ty, tx, (c + cc) % 2), z,
        )

    def dir_step(i, narrow):
        r, dest = dir_of(i)
        gather(dest, r, 72 + i * 2, narrow)
        dir_copy(i, narrow).start()

        @pl.when(i < 18)
        def _():
            mid_copy(i, narrow).wait_recv()
            for cc in range(2):
                fwd_copy(i, cc, narrow).start()

    def first_mid(i, carry):
        mid_step(i, False)
        return carry

    lax.fori_loop(0, 18, first_mid, 0)

    def two(q):
        return pl.ds(q * 2, 2)

    def mine(q):
        return pl.ds(z * 16 + q * 2, 2)

    def z_wait(q, src, sems):
        remote(
            feat.at[pl.ds(0, 2)], zrecv.at[src, two(q)], z_send.at[0],
            sems.at[q * 4 + src], d, src,
        ).wait_recv()

    def mix(q, sems, col):
        zrecv[z, two(q)] = feat[mine(q)]
        for k in range(1, 4):
            z_wait(q, (z + k) % 4, sems)
        lhs = [zrecv[s, two(q)].reshape(256, 256) for s in range(4)]
        res = []
        for b in (0, 2):
            total = None
            for s in range(4):
                w = [wbuf[b + e, s * 256 : (s + 1) * 256, col : col + N] for e in range(2)]
                p = jnp.dot(lhs[s], jnp.concatenate(w, axis=1), preferred_element_type=f32)
                total = p if total is None else total + p
            res.append(total)
        return res

    def back_copy(q, k, buf, sems):
        dst = (z + k) % 4
        return remote(
            nbuf.at[dst, two(q)], buf.at[mine(q)], n_send.at[q * 3 + k - 1],
            sems.at[q * 4 + z], d, dst,
        )

    def back_wait(q, src, buf, sems):
        remote(
            nbuf.at[0, two(q)], buf.at[pl.ds(src * 16 + q * 2, 2)], n_send.at[0],
            sems.at[q * 4 + src], d, src,
        ).wait_recv()

    def premix_step(q, carry):
        res = mix(q, z_recv, N)
        for b in range(4):
            half = res[b // 2][:, (b % 2) * N : (b % 2 + 1) * N]
            nbuf[b, two(q)] = half.astype(bf16).reshape(2, T, N)
        for k in ZORD:
            back_copy(q, k, zb, zb_recv).start()
        zb[mine(q)] = nbuf[z, two(q)]
        return carry

    def first_dir(i, carry):
        dir_step(i, False)

        @pl.when(i % 5 == 3)
        def _():
            premix_step(i // 5, 0)

        return carry

    w_wait(1)
    lax.fori_loop(0, 26, first_dir, 0)
    lax.fori_loop(5, 6, premix_step, 0)

    def tile_sum(slot, tt, idx, cnt, zero, t, buf):
        total = None
        at = [jnp.where(k < cnt[0, t], idx[k, t], zero) for k in range(4)]
        for k in (0, 2):
            lhs = jnp.concatenate([abuf[slot, tt, k], abuf[slot, tt, k + 1]], axis=1)
            rhs = jnp.concatenate([buf[at[k]], buf[at[k + 1]]], axis=0)
            p = jnp.dot(lhs, rhs, preferred_element_type=f32)
            total = p if total is None else total + p
        return total

    def stream(vals, chunk_of, use):
        def step(s, carry):
            slot = s % SLOTS
            a_chunk(vals, chunk_of(s), slot).wait()
            use(s, slot)

            @pl.when(s + SLOTS < 32)
            def _():
                a_chunk(vals, chunk_of(s + SLOTS), slot).start()

            return carry

        lax.fori_loop(0, 32, step, 0)

    def ahead(vals, chunk_of):
        for s in range(SLOTS):
            a_chunk(vals, chunk_of(s), s).start()

    def t_rows(t):
        return pl.ds(pl.multiple_of(t * T, T), T)

    def in_order(s):
        return s

    def own_a(s, slot):
        for tt in range(2):
            t = s * 2 + tt
            acc[t_rows(t), :] = tile_sum(slot, tt, lidx, lcnt, 64, t, feat)

    stream(lval, in_order, own_a)
    lax.fori_loop(6, 8, premix_step, 0)
    for k in range(1, 4):
        w_copy(k, 0).start()
        bias_copy(k).start()

    def halo_chunk(s):
        return z_plane(s % 4) * 8 + s // 4

    ahead(hval, halo_chunk)

    def zb_wait(q, carry):
        for k in range(1, 4):
            back_wait(q, (z + k) % 4, zb, zb_recv)
        return carry

    lax.fori_loop(0, 8, zb_wait, 0)

    def rebuild(i, carry):
        mixed = []
        for u in range(8):
            rows = zb[i * 8 + u]
            turned = pltpu.roll(rows.astype(f32), 64, 1).astype(bf16)
            both = jnp.concatenate([rows, turned], axis=0)
            mixed.append(jnp.dot(merge, both, preferred_element_type=f32).astype(bf16))
        for u in range(8):
            tab[pl.ds(pl.multiple_of(i * 1024 + u * T, T), T)] = mixed[u].reshape(T, 2, 128)
        return carry

    lax.fori_loop(0, 8, rebuild, 0)

    def second_mid(i, carry):
        mid_copy(i, False).wait_send()
        mid_step(i, True)
        return carry

    lax.fori_loop(0, SPLIT, second_mid, 0)

    recv[pl.ds(d * 4, 4)] = jnp.zeros((4, T, 256), bf16)
    recv2[pl.ds(d * 4, 4)] = jnp.zeros((4, T, N), bf16)

    def z_sent(s, carry):
        z_copy(s // 3, s % 3, z_recv).wait_send()
        return carry

    lax.fori_loop(0, 24, z_sent, 0)

    def arrive(k, narrow):
        src = (d + k) % 32
        for r in range(2):
            dst, sem = fin_at(src, r, narrow)
            remote(sent(0, 2, narrow), dst, dir_send.at[0], sem, d, z).wait_recv()

    def first_arrive(k, carry):
        arrive(k, False)
        return carry

    lax.fori_loop(1, 32, first_arrive, 0)

    def halo_a(s, slot):
        chunk = halo_chunk(s)
        for tt in range(2):
            t = chunk * 2 + tt
            total = acc[t_rows(t), :] + tile_sum(slot, tt, hidx, hcnt, d * 4, t, recv)
            feat[t] = total.astype(bf16)

        @pl.when(s % 4 < 3)
        def _():
            z_copy(s // 4, s % 4, z_recv2).start()

    stream(hval, halo_chunk, halo_a)
    ahead(lval, in_order)

    lax.fori_loop(SPLIT, 18, second_mid, 0)

    def first_sent(i, carry):
        for cc in range(2):
            fwd_copy(i, cc, False).wait_send()
        return carry

    lax.fori_loop(0, 18, first_sent, 0)

    def second_dir(i, carry):
        dir_copy(i, False).wait_send()
        dir_step(i, True)
        return carry

    lax.fori_loop(0, 26, second_dir, 0)

    def own_b(s, slot):
        for tt in range(2):
            t = s * 2 + tt
            acc[t_rows(t), 0:N] = tile_sum(slot, tt, lidx, lcnt, 64, t, zb)

    stream(lval, in_order, own_b)
    ahead(hval, in_order)

    def back_sent(q, carry):
        for k in range(1, 4):
            back_copy(q, k, zb, zb_recv).wait_send()
        return carry

    lax.fori_loop(0, 8, back_sent, 0)

    def as_row(col):
        return jnp.broadcast_to(col, (256, 128)).T[0:1, :]

    def pa_copy(q, k):
        dst = (z + k) % 4
        return remote(
            pa.at[z, q], pa.at[z, q], pa_send.at[q * 3 + k - 1], pa_recv.at[q * 4 + z], d, dst
        )

    def mix_step(q, carry):
        res = mix(q, z_recv2, 0)
        power = None
        for b in (0, 2):
            bias = jnp.concatenate([bbuf[b], bbuf[b + 1]], axis=1)
            keep = jnp.concatenate([bias[:, 0:N], bias[:, 256 : 256 + N]], axis=1)
            act = jnp.maximum(res[b // 2] + keep.astype(f32), 0.0)
            p = jnp.sum(act * act, axis=1, keepdims=True)
            power = p if power is None else power + p
            for e in range(2):
                half = act[:, e * N : (e + 1) * N]
                nbuf[b + e, two(q)] = half.astype(bf16).reshape(2, T, N)
        pa[z, q] = as_row(power)
        for k in ZORD:
            back_copy(q, k, ya, o_recv).start()
            pa_copy(q, k).start()
        ya[mine(q)] = nbuf[z, two(q)]
        return carry

    w_wait(0)
    for k in range(1, 4):
        src = (z + k) % 4
        remote(bbuf.at[src], bbuf.at[src], b_send.at[0], b_recv.at[src], d, src).wait_recv()
    lax.fori_loop(0, 8, mix_step, 0)

    def second_arrive(k, carry):
        arrive(k, True)
        return carry

    lax.fori_loop(1, 32, second_arrive, 0)

    def halo_b(s, slot):
        power = []
        for tt in range(2):
            t = s * 2 + tt
            total = acc[t_rows(t), 0:N] + tile_sum(slot, tt, hidx, hcnt, d * 4, t, recv2)
            act = jnp.maximum(total + bbuf[z][:, N : 2 * N].astype(f32), 0.0)
            acc[t_rows(t), 0:N] = act
            power.append(jnp.sum(act * act, axis=1, keepdims=True))
        pb[z, s] = as_row(jnp.concatenate(power, axis=0))

    stream(hval, in_order, halo_b)

    def pb_copy(k):
        return remote(pb.at[z], pb.at[z], pb_send.at[k - 1], pb_recv.at[z], d, (z + k) % 4)

    for k in range(1, 4):
        pb_copy(k).start()
    for k in range(1, 4):
        src = (z + k) % 4
        remote(pb.at[src], pb.at[src], pb_send.at[0], pb_recv.at[src], d, src).wait_recv()

    part[...] = jnp.zeros_like(part)

    def norm_step(q, carry):
        for k in range(1, 4):
            src = (z + k) % 4
            back_wait(q, src, ya, o_recv)
            remote(pa.at[src, q], pa.at[src, q], pa_send.at[0], pa_recv.at[q * 4 + src], d, src).wait_recv()
        sums = [[None, None], [None, None]]
        for p in range(4):
            chunk = p * 8 + q
            power = pa[p, q] + pb[0, chunk] + pb[1, chunk] + pb[2, chunk] + pb[3, chunk]
            scale = jnp.broadcast_to(lax.rsqrt(power * (1.0 / 1024.0) + epsilon), (128, 256)).T
            at = pl.ds(p * 16 + q * 2, 2)
            acts = (
                ya[at].reshape(256, N).astype(f32),
                acc[pl.ds(pl.multiple_of(chunk * 256, 256), 256), 0:N],
            )
            for h in range(2):
                scaled = acts[h] * scale
                out[at, :, h * N : (h + 1) * N] = scaled.astype(bf16).reshape(2, T, N)
                for e, v in enumerate((scaled, scaled * scaled)):
                    v = jnp.sum(v, axis=0, keepdims=True)
                    sums[h][e] = v if sums[h][e] is None else sums[h][e] + v
        for h in range(2):
            for e in range(2):
                part[e : e + 1, h * N : (h + 1) * N] += sums[h][e]
        return carry

    lax.fori_loop(0, 8, norm_step, 0)

    me = x * 2 + c

    def s1_copy(k):
        to = (me + k) % 8
        return remote(s1.at[me], s1.at[me], s1_send.at[k - 1], s1_recv.at[me], y * 8 + to, z)

    def s2_copy(k):
        to = dom_of((y + k) % 4, x, c)
        return remote(s2.at[y], s2.at[y], s2_send.at[k - 1], s2_recv.at[y], to, z)

    s1[me] = part[...]
    for k in range(1, 8):
        s1_copy(k).start()
    for k in range(1, 8):
        src = (me + k) % 8
        remote(s1.at[src], s1.at[src], s1_send.at[0], s1_recv.at[src], d, z).wait_recv()
    total = s1[0]
    for k in range(1, 8):
        total = total + s1[k]
    s2[y] = total
    for k in range(1, 4):
        s2_copy(k).start()

    def last_mid(i, carry):
        mid_copy(i, True).wait_send()
        for cc in range(2):
            fwd_copy(i, cc, True).wait_send()
        return carry

    lax.fori_loop(0, 18, last_mid, 0)

    def last_dir(i, carry):
        dir_copy(i, True).wait_send()
        return carry

    lax.fori_loop(0, 26, last_dir, 0)

    def last_z(s, carry):
        z_copy(s // 3, s % 3, z_recv2).wait_send()
        return carry

    lax.fori_loop(0, 24, last_z, 0)

    def last_back(q, carry):
        for k in range(1, 4):
            back_copy(q, k, ya, o_recv).wait_send()
            pa_copy(q, k).wait_send()
        return carry

    lax.fori_loop(0, 8, last_back, 0)
    for k in range(1, 4):
        for h in range(2):
            w_copy(k, h).wait_send()
            w_give(k, h).wait_send()
        bias_copy(k).wait_send()
        pb_copy(k).wait_send()
    for k in range(1, 8):
        s1_copy(k).wait_send()
    for k in range(1, 4):
        src = (y + k) % 4
        remote(s2.at[src], s2.at[src], s2_send.at[0], s2_recv.at[src], d, z).wait_recv()
        s2_copy(k).wait_send()
    sums = (s2[0] + s2[1] + s2[2] + s2[3]) * (1.0 / 262144.0)
    mean = sums[0:1, :]
    stats[0:1, :] = mean
    stats[1:2, :] = sums[1:2, :] - mean * mean


def on_device(
    features, weight, out_bias, local_index, local_count, local_vals,
    halo_index, halo_count, halo_vals, send_rows, send_count,
):
    smem = pl.BlockSpec(memory_space=pltpu.SMEM)
    hbm = pl.BlockSpec(memory_space=pl.ANY)
    bf16, f32 = jnp.bfloat16, jnp.float32
    V = pltpu.VMEM
    dma = lambda n: pltpu.SemaphoreType.DMA((n,))
    out, stats = pl.pallas_call(
        layer,
        out_shape=(V((64, T, 256), bf16), V((2, 256), f32)),
        in_specs=[smem] * 6 + [hbm] * 5,
        out_specs=(pl.BlockSpec(memory_space=V), pl.BlockSpec(memory_space=V)),
        scratch_shapes=[
            V((65, T, 256), bf16),
            V((8192, 2, 128), bf16),
            V((HALF, 2, 128), bf16),
            V((72 + 26 * 2, T, 256), bf16),
            V((72, T, 256), bf16),
            V((72, T, N), bf16),
            V((128, T, 256), bf16),
            V((128, T, N), bf16),
            V((8192, 256), f32),
            V((SLOTS, 2, 4, 128, 128), bf16),
            V((4, 16, T, 256), bf16),
            V((4, 1024, 256), bf16),
            V((4, 1, 256), bf16),
            V((4, 16, T, N), bf16),
            V((65, T, N), bf16),
            V((64, T, N), bf16),
            V((4, 8, 1, 256), f32),
            V((4, 32, 1, 256), f32),
            V((2, 256), f32),
            V((8, 2, 256), f32),
            V((4, 2, 256), f32),
            dma(3), dma(SLOTS), dma(6), dma(8), dma(6), dma(8), dma(3), dma(4),
            dma(18), dma(18), dma(18), dma(26), dma(36), dma(64), dma(64),
            dma(24), dma(32), dma(32), dma(24), dma(32), dma(32), dma(24), dma(32), dma(3), dma(4),
            dma(7), dma(8), dma(3), dma(4),
        ],
        compiler_params=pltpu.CompilerParams(
            collective_id=0, has_side_effects=True, vmem_limit_bytes=62000000
        ),
        name="layer",
    )(
        send_rows.reshape(-1), send_count, local_index[0].T, local_count, halo_index[0].T, halo_count,
        features.reshape(64, T, 256), weight, out_bias.reshape(1, 256), local_vals[0], halo_vals[0],
    )
    return out.reshape(8192, 256), stats


def solution(mesh):
    in_specs = (
        P("dom", "col"), P(None, "col"), P("col"),
        P("dom", None, None), P("dom", None), P("dom", None, None, None, None),
        P("dom", None, None), P("dom", None), P("dom", None, None, None, None),
        P("dom", None, None), P("dom", None),
    )
    return jax.shard_map(
        on_device, mesh=mesh, in_specs=in_specs,
        out_specs=(P("dom", "col"), P(None, "col")), check_vma=False,
    )
```

time: 214 us -> 202 us (0.944)
  Pallas kernels: 205 us -> 194 us
    pallas_call x1, Pallas kernels: 205 us -> 194 us  [on_device(): pl.pallas_call(layer, out_shape=(V((64, T, 256), bf16), V((2, 256), f32))...]
    unnamed x4 -> x3, local copies, waits for them, and re-layouts: 5.05 us -> 4.08 us
where the time goes in v3:
time: 202 us; the launch traced here: 200 us
  Pallas kernels  194 us (96%)
  local copies, waits for them, and re-layouts  5.3 us (3%)
    pallas_call x1, Pallas kernels, on_device(): pl.pallas_call(layer, out_shape=(V((64, T, 256), bf16), V((2, 256), f32))...  194 us
    unnamed x3, local copies, waits for them, and re-layouts  4.08 us

profile of v3, /device:TPU:6, one launch (start us, length us, event | category | flops | bytes accessed | tf_op | source)
XLA Modules:
  0.0 200.1 jit_solution(8977323541219979895)
XLA Ops:
  0.6 1.2 reshape.18.bias_hbm
  1.9 1.5 copy.13
  3.3 194.2 %layer.1 = (bf16[64,128,256]{2,1,0:T(8,128)(2,1)S(1)}, f32[2,256]{1,0:T(2,128)S(1)}) custom-call(s32[16384]{0:T(1024)} %bitcast.16, s32[1,32]{1,0:T(1,128)} %scnt.1, s32[4,64]{1,0:T(4,128)} %bitcast.18, s32[1,64]{1,0:T(1,128)} %lcnt.1, s32[4,64]{1,0:T(4,128)} %bitcast.19, s32[1,64]{1,0:T(1,128)} %hcnt.1, bf16[64,128,256]{2,1,0:T(8,128)(2,1)} %bitcast.15, ...), custom_call_target="tpu_custom_call" | custom-call | tf_op jit(solution)/shard_map/layer/pallas_call | solution.py:620
  197.5 2.0 %copy.16 = bf16[8192,256]{1,0:T(8,128)(2,1)} copy(bf16[8192,256]{1,0:T(8,128)(2,1)S(1)} %bitcast.12) | data formatting | bytes 8388608
  199.5 0.6 copy.17

commit v4 on v3

--- a/solution.py
+++ b/solution.py
@@ -12,6 +12,7 @@
 HALF = 256
 G = 64
 ZORD = (2, 1, 3)
+LATE = 6
 SPLIT = 12
 SLOTS = 4
 N = 128
@@ -22,14 +23,14 @@
 
 
 def layer(
-    sidx, scnt, lidx, lcnt, hidx, hcnt, feat_hbm, w_hbm, bias_hbm, lval, hval,
+    sidx_hbm, scnt, lidx, lcnt, hidx, hcnt, feat_hbm, w_hbm, bias_hbm, lval, hval,
     out, stats,
-    feat, tab, stage, send, mid, mid2, recv, recv2, acc, abuf, zrecv, wbuf, bbuf, nbuf,
-    zb, ya, pa, pb, part, s1, s2,
-    in_sem, a_sem, w_send, w_recv, wg_send, wg_recv, b_send, b_recv,
+    sidx, feat, tab, stage, send, mid, mid2, recv, recv2, acc, abuf, zrecv, wbuf, bbuf, b_own, nbuf,
+    zb, ya, pa, pb, part, s1,
+    in_sem, idx_sem, a_sem, w_send, w_recv, wg_send, wg_recv, b_send, b_recv,
     mid_send, mid_recv, mid_recv2, dir_send, fwd_send, fin_recv, fin_recv2,
     z_send, z_recv, z_recv2, n_send, zb_recv, o_recv, pa_send, pa_recv, pb_send, pb_recv,
-    s1_send, s1_recv, s2_send, s2_recv,
+    s1_send, s1_recv,
 ):
     f32, bf16 = jnp.float32, jnp.bfloat16
     d = lax.axis_index("dom")
@@ -47,31 +48,36 @@
             device_id={"dom": dom, "col": col}, device_id_type=MESH,
         )
 
+    def feat_in(i):
+        tiles = pl.ds(i * 8, 8)
+        return pltpu.make_async_copy(feat_hbm.at[tiles], feat.at[tiles], in_sem.at[4 + i])
+
+    for i in range(8):
+        feat_in(i).start()
+
+    def idx_in(p):
+        return pltpu.make_async_copy(sidx_hbm.at[p], sidx.at[pl.ds(p * 512, 512)], idx_sem.at[p])
+
+    for p in range(32):
+        idx_in(p).start()
+    w_in = pltpu.make_async_copy(w_hbm, wbuf.at[z], in_sem.at[1])
+    w_in.start()
+    b_in = pltpu.make_async_copy(bias_hbm, b_own, in_sem.at[2])
+    b_in.start()
+
+    def a_chunk(vals, chunk, slot):
+        return pltpu.make_async_copy(vals.at[pl.ds(chunk * 2, 2)], abuf.at[slot], a_sem.at[slot])
+
+    for s in range(SLOTS):
+        a_chunk(lval, s, s).start()
+
     barrier = pltpu.get_barrier_semaphore()
-    peers = []
-    for k in range(1, 4):
-        for cc in range(2):
-            peers.append((dom_of(y, (x + k) % 4, cc), z))
-            peers.append((dom_of((y + k) % 4, x, cc), z))
-        peers.append((d, (z + k) % 4))
-    peers.append((dom_of(y, x, 1 - c), z))
+    peers = [((d + k) % 32, z) for k in range(1, 32)] + [(d, (z + k) % 4) for k in range(1, 4)]
     for dom, col in peers:
         pl.semaphore_signal(
             barrier, inc=1, device_id={"dom": dom, "col": col}, device_id_type=MESH
         )
 
-    feat_in = pltpu.make_async_copy(feat_hbm, feat.at[pl.ds(0, 64)], in_sem.at[0])
-    feat_in.start()
-    w_in = pltpu.make_async_copy(w_hbm, wbuf.at[z], in_sem.at[1])
-    w_in.start()
-    b_in = pltpu.make_async_copy(bias_hbm, bbuf.at[z], in_sem.at[2])
-    b_in.start()
-
-    def a_chunk(vals, chunk, slot):
-        return pltpu.make_async_copy(vals.at[pl.ds(chunk * 2, 2)], abuf.at[slot], a_sem.at[slot])
-
-    for s in range(SLOTS):
-        a_chunk(lval, s, s).start()
 
     row = lax.broadcasted_iota(jnp.int32, (256, 256), 0)
     lane = lax.broadcasted_iota(jnp.int32, (256, 256), 1)
@@ -84,21 +90,30 @@
 
     feat[64] = jnp.zeros((T, 256), bf16)
     zb[64] = jnp.zeros((T, N), bf16)
-    feat_in.wait()
-
     def build(i, carry):
+        feat_in(i).wait()
         mixed = []
-        for u in range(8):
-            rows = feat[i * 8 + u]
-            both = jnp.concatenate([rows[:, :128], rows[:, 128:]], axis=0)
+        for u in range(0, 8, 2):
+            rows = [feat[i * 8 + u + e] for e in range(2)]
+            both = jnp.concatenate(
+                [
+                    jnp.concatenate([rows[0][:, :128], rows[1][:, :128]], axis=1),
+                    jnp.concatenate([rows[0][:, 128:], rows[1][:, 128:]], axis=1),
+                ],
+                axis=0,
+            )
             mixed.append(jnp.dot(merge, both, preferred_element_type=f32).astype(bf16))
         for u in range(8):
-            tab[pl.ds(pl.multiple_of(i * 1024 + u * T, T), T)] = mixed[u].reshape(T, 2, 128)
+            half = mixed[u // 2][:, u % 2 * 128 : (u % 2 + 1) * 128]
+            tab[pl.ds(pl.multiple_of(i * 1024 + u * T, T), T)] = half.reshape(T, 2, 128)
         return carry
 
     lax.fori_loop(0, 8, build, 0)
     w_in.wait()
     b_in.wait()
+    bbuf[z] = b_own[...].reshape(1, 256)
+    for p in range(32):
+        idx_in(p).wait()
     pl.semaphore_wait(barrier, len(peers))
 
     other = dom_of(y, x, 1 - c)
@@ -296,14 +311,15 @@
     def first_dir(i, carry):
         dir_step(i, False)
 
-        @pl.when(i % 5 == 3)
+        @pl.when(i % 5 == 4)
         def _():
             premix_step(i // 5, 0)
 
         return carry
 
+    lax.fori_loop(0, 3, first_dir, 0)
     w_wait(1)
-    lax.fori_loop(0, 26, first_dir, 0)
+    lax.fori_loop(3, 26, first_dir, 0)
     lax.fori_loop(5, 6, premix_step, 0)
 
     def tile_sum(slot, tt, idx, cnt, zero, t, buf):
@@ -365,13 +381,14 @@
 
     def rebuild(i, carry):
         mixed = []
-        for u in range(8):
-            rows = zb[i * 8 + u]
-            turned = pltpu.roll(rows.astype(f32), 64, 1).astype(bf16)
-            both = jnp.concatenate([rows, turned], axis=0)
+        for u in range(0, 8, 2):
+            rows = jnp.concatenate([zb[i * 8 + u], zb[i * 8 + u + 1]], axis=1)
+            turned = [pltpu.roll(zb[i * 8 + u + e].astype(f32), 64, 1).astype(bf16) for e in range(2)]
+            both = jnp.concatenate([rows, jnp.concatenate(turned, axis=1)], axis=0)
             mixed.append(jnp.dot(merge, both, preferred_element_type=f32).astype(bf16))
         for u in range(8):
-            tab[pl.ds(pl.multiple_of(i * 1024 + u * T, T), T)] = mixed[u].reshape(T, 2, 128)
+            half = mixed[u // 2][:, u % 2 * 128 : (u % 2 + 1) * 128]
+            tab[pl.ds(pl.multiple_of(i * 1024 + u * T, T), T)] = half.reshape(T, 2, 128)
         return carry
 
     lax.fori_loop(0, 8, rebuild, 0)
@@ -449,8 +466,8 @@
 
     lax.fori_loop(0, 8, back_sent, 0)
 
-    def as_row(col):
-        return jnp.broadcast_to(col, (256, 128)).T[0:1, :]
+    def power_row(square):
+        return jnp.sum(square.T, axis=0, keepdims=True)
 
     def pa_copy(q, k):
         dst = (z + k) % 4
@@ -465,12 +482,12 @@
             bias = jnp.concatenate([bbuf[b], bbuf[b + 1]], axis=1)
             keep = jnp.concatenate([bias[:, 0:N], bias[:, 256 : 256 + N]], axis=1)
             act = jnp.maximum(res[b // 2] + keep.astype(f32), 0.0)
-            p = jnp.sum(act * act, axis=1, keepdims=True)
-            power = p if power is None else power + p
             for e in range(2):
                 half = act[:, e * N : (e + 1) * N]
+                p = half * half
+                power = p if power is None else power + p
                 nbuf[b + e, two(q)] = half.astype(bf16).reshape(2, T, N)
-        pa[z, q] = as_row(power)
+        pa[z, q] = power_row(power)
         for k in ZORD:
             back_copy(q, k, ya, o_recv).start()
             pa_copy(q, k).start()
@@ -481,7 +498,7 @@
     for k in range(1, 4):
         src = (z + k) % 4
         remote(bbuf.at[src], bbuf.at[src], b_send.at[0], b_recv.at[src], d, src).wait_recv()
-    lax.fori_loop(0, 8, mix_step, 0)
+    lax.fori_loop(0, LATE, mix_step, 0)
 
     def second_arrive(k, carry):
         arrive(k, True)
@@ -496,8 +513,8 @@
             total = acc[t_rows(t), 0:N] + tile_sum(slot, tt, hidx, hcnt, d * 4, t, recv2)
             act = jnp.maximum(total + bbuf[z][:, N : 2 * N].astype(f32), 0.0)
             acc[t_rows(t), 0:N] = act
-            power.append(jnp.sum(act * act, axis=1, keepdims=True))
-        pb[z, s] = as_row(jnp.concatenate(power, axis=0))
+            power.append(act * act)
+        pb[z, s] = power_row(jnp.concatenate(power, axis=0))
 
     stream(hval, in_order, halo_b)
 
@@ -506,6 +523,7 @@
 
     for k in range(1, 4):
         pb_copy(k).start()
+    lax.fori_loop(LATE, 8, mix_step, 0)
     for k in range(1, 4):
         src = (z + k) % 4
         remote(pb.at[src], pb.at[src], pb_send.at[0], pb_recv.at[src], d, src).wait_recv()
@@ -540,28 +558,16 @@
 
     lax.fori_loop(0, 8, norm_step, 0)
 
-    me = x * 2 + c
-
     def s1_copy(k):
-        to = (me + k) % 8
-        return remote(s1.at[me], s1.at[me], s1_send.at[k - 1], s1_recv.at[me], y * 8 + to, z)
-
-    def s2_copy(k):
-        to = dom_of((y + k) % 4, x, c)
-        return remote(s2.at[y], s2.at[y], s2_send.at[k - 1], s2_recv.at[y], to, z)
-
-    s1[me] = part[...]
-    for k in range(1, 8):
+        return remote(s1.at[d], s1.at[d], s1_send.at[k], s1_recv.at[d], (d + k) % 32, z)
+
+    s1[d] = part[...]
+
+    def s1_start(k, carry):
         s1_copy(k).start()
-    for k in range(1, 8):
-        src = (me + k) % 8
-        remote(s1.at[src], s1.at[src], s1_send.at[0], s1_recv.at[src], d, z).wait_recv()
-    total = s1[0]
-    for k in range(1, 8):
-        total = total + s1[k]
-    s2[y] = total
-    for k in range(1, 4):
-        s2_copy(k).start()
+        return carry
+
+    lax.fori_loop(1, 32, s1_start, 0)
 
     def last_mid(i, carry):
         mid_copy(i, True).wait_send()
@@ -596,13 +602,15 @@
             w_give(k, h).wait_send()
         bias_copy(k).wait_send()
         pb_copy(k).wait_send()
-    for k in range(1, 8):
+
+    def s1_wait(k, carry):
+        src = (d + k) % 32
+        remote(s1.at[src], s1.at[src], s1_send.at[0], s1_recv.at[src], d, z).wait_recv()
         s1_copy(k).wait_send()
-    for k in range(1, 4):
-        src = (y + k) % 4
-        remote(s2.at[src], s2.at[src], s2_send.at[0], s2_recv.at[src], d, z).wait_recv()
-        s2_copy(k).wait_send()
-    sums = (s2[0] + s2[1] + s2[2] + s2[3]) * (1.0 / 262144.0)
+        return carry
+
+    lax.fori_loop(1, 32, s1_wait, 0)
+    sums = jnp.sum(s1[...], axis=0) * (1.0 / 262144.0)
     mean = sums[0:1, :]
     stats[0:1, :] = mean
     stats[1:2, :] = sums[1:2, :] - mean * mean
@@ -620,9 +628,10 @@
     out, stats = pl.pallas_call(
         layer,
         out_shape=(V((64, T, 256), bf16), V((2, 256), f32)),
-        in_specs=[smem] * 6 + [hbm] * 5,
+        in_specs=[hbm] + [smem] * 5 + [hbm] * 5,
         out_specs=(pl.BlockSpec(memory_space=V), pl.BlockSpec(memory_space=V)),
         scratch_shapes=[
+            pltpu.SMEM((16384,), jnp.int32),
             V((65, T, 256), bf16),
             V((8192, 2, 128), bf16),
             V((HALF, 2, 128), bf16),
@@ -636,26 +645,26 @@
             V((4, 16, T, 256), bf16),
             V((4, 1024, 256), bf16),
             V((4, 1, 256), bf16),
+            V((256,), bf16),
             V((4, 16, T, N), bf16),
             V((65, T, N), bf16),
             V((64, T, N), bf16),
             V((4, 8, 1, 256), f32),
             V((4, 32, 1, 256), f32),
             V((2, 256), f32),
-            V((8, 2, 256), f32),
-            V((4, 2, 256), f32),
-            dma(3), dma(SLOTS), dma(6), dma(8), dma(6), dma(8), dma(3), dma(4),
+            V((32, 2, 256), f32),
+            dma(12), dma(32), dma(SLOTS), dma(6), dma(8), dma(6), dma(8), dma(3), dma(4),
             dma(18), dma(18), dma(18), dma(26), dma(36), dma(64), dma(64),
             dma(24), dma(32), dma(32), dma(24), dma(32), dma(32), dma(24), dma(32), dma(3), dma(4),
-            dma(7), dma(8), dma(3), dma(4),
+            dma(32), dma(32),
         ],
         compiler_params=pltpu.CompilerParams(
             collective_id=0, has_side_effects=True, vmem_limit_bytes=62000000
         ),
         name="layer",
     )(
-        send_rows.reshape(-1), send_count, local_index[0].T, local_count, halo_index[0].T, halo_count,
-        features.reshape(64, T, 256), weight, out_bias.reshape(1, 256), local_vals[0], halo_vals[0],
+        send_rows[0], send_count, local_index[0].T, local_count, halo_index[0].T, halo_count,
+        features.reshape(64, T, 256), weight, out_bias, local_vals[0], halo_vals[0],
     )
     return out.reshape(8192, 256), stats
 

time: 202 us -> 195 us (0.965)
  Pallas kernels: 194 us -> 189 us
  local copies, waits for them, and re-layouts: 5.3 us -> 2.59 us
    pallas_call x1, Pallas kernels: 194 us -> 189 us  [on_device(): pl.pallas_call(layer, out_shape=(V((64, T, 256), bf16), V((2, 256), f32))...]
    unnamed x3 -> x2, local copies, waits for them, and re-layouts: 4.08 us -> 2.59 us
where the time goes in v4:
time: 195 us; the launch traced here: 192 us
  Pallas kernels  189 us (97%)
  local copies, waits for them, and re-layouts  2.59 us (1%)
    pallas_call x1, Pallas kernels, on_device(): pl.pallas_call(layer, out_shape=(V((64, T, 256), bf16), V((2, 256), f32))...  189 us

profile of v4, /device:TPU:6, one launch (start us, length us, event | category | flops | bytes accessed | tf_op | source)
XLA Modules:
  0.0 192.3 jit_solution(16310580564647007991)
XLA Ops:
  0.6 189.0 %layer.1 = (bf16[64,128,256]{2,1,0:T(8,128)(2,1)S(1)}, f32[2,256]{1,0:T(2,128)S(1)}) custom-call(s32[32,512]{1,0:T(8,128)} %bitcast.15, s32[1,32]{1,0:T(1,128)} %scnt.1, s32[4,64]{1,0:T(4,128)} %bitcast.16, s32[1,64]{1,0:T(1,128)} %lcnt.1, s32[4,64]{1,0:T(4,128)} %bitcast.17, s32[1,64]{1,0:T(1,128)} %hcnt.1, bf16[64,128,256]{2,1,0:T(8,128)(2,1)} %bitcast.14, ...), custom_call_target="tpu_custom_call" | custom-call | tf_op jit(solution)/shard_map/layer/pallas_call | solution.py:628
  189.7 2.0 %copy.15 = bf16[8192,256]{1,0:T(8,128)(2,1)} copy(bf16[8192,256]{1,0:T(8,128)(2,1)S(1)} %bitcast.11) | data formatting | bytes 8388608
  191.7 0.6 copy.16

commit v5 on v4

--- a/solution.py
+++ b/solution.py
@@ -14,6 +14,8 @@
 ZORD = (2, 1, 3)
 LATE = 6
 SPLIT = 12
+SMALL = 2.0**-8
+TOP = 1e38
 SLOTS = 4
 N = 128
 
@@ -185,7 +187,7 @@
     def mid_of(i):
         r = i % 2
         j = i // 2
-        return r, 1 + (j * 2) % 3, 1 + j // 3
+        return r, 1 + (j + 1) % 3, 1 + j // 3
 
     def sent(at, n, narrow):
         return send.at[pl.ds(at, n), :, pl.ds(0, 128)] if narrow else send.at[pl.ds(at, n)]
@@ -270,7 +272,7 @@
             sems.at[q * 4 + src], d, src,
         ).wait_recv()
 
-    def mix(q, sems, col):
+    def mix(q, sems, col, scale=None):
         zrecv[z, two(q)] = feat[mine(q)]
         for k in range(1, 4):
             z_wait(q, (z + k) % 4, sems)
@@ -280,7 +282,10 @@
             total = None
             for s in range(4):
                 w = [wbuf[b + e, s * 256 : (s + 1) * 256, col : col + N] for e in range(2)]
-                p = jnp.dot(lhs[s], jnp.concatenate(w, axis=1), preferred_element_type=f32)
+                w = jnp.concatenate(w, axis=1)
+                if scale is not None:
+                    w = w * jnp.asarray(scale, bf16)
+                p = jnp.dot(lhs[s], w, preferred_element_type=f32)
                 total = p if total is None else total + p
             res.append(total)
         return res
@@ -299,7 +304,7 @@
         ).wait_recv()
 
     def premix_step(q, carry):
-        res = mix(q, z_recv, N)
+        res = mix(q, z_recv, N, SMALL)
         for b in range(4):
             half = res[b // 2][:, (b % 2) * N : (b % 2 + 1) * N]
             nbuf[b, two(q)] = half.astype(bf16).reshape(2, T, N)
@@ -481,7 +486,7 @@
         for b in (0, 2):
             bias = jnp.concatenate([bbuf[b], bbuf[b + 1]], axis=1)
             keep = jnp.concatenate([bias[:, 0:N], bias[:, 256 : 256 + N]], axis=1)
-            act = jnp.maximum(res[b // 2] + keep.astype(f32), 0.0)
+            act = jnp.clip(res[b // 2] + keep.astype(f32), 0.0, TOP)
             for e in range(2):
                 half = act[:, e * N : (e + 1) * N]
                 p = half * half
@@ -511,7 +516,7 @@
         for tt in range(2):
             t = s * 2 + tt
             total = acc[t_rows(t), 0:N] + tile_sum(slot, tt, hidx, hcnt, d * 4, t, recv2)
-            act = jnp.maximum(total + bbuf[z][:, N : 2 * N].astype(f32), 0.0)
+            act = jnp.maximum(total * (1.0 / SMALL) + bbuf[z][:, N : 2 * N].astype(f32), 0.0)
             acc[t_rows(t), 0:N] = act
             power.append(act * act)
         pb[z, s] = power_row(jnp.concatenate(power, axis=0))

time: 195 us -> 194 us (level)
  no operation moved by 1% of the time
where the time goes in v5:
time: 194 us; the launch traced here: 192 us
  Pallas kernels  188 us (97%)
  local copies, waits for them, and re-layouts  2.59 us (1%)
    pallas_call x1, Pallas kernels, on_device(): pl.pallas_call(layer, out_shape=(V((64, T, 256), bf16), V((2, 256), f32))...  188 us

profile of v5, /device:TPU:6, one launch (start us, length us, event | category | flops | bytes accessed | tf_op | source)
XLA Modules:
  0.0 191.6 jit_solution(12033613918699538085)
XLA Ops:
  0.6 188.3 %layer.1 = (bf16[64,128,256]{2,1,0:T(8,128)(2,1)S(1)}, f32[2,256]{1,0:T(2,128)S(1)}) custom-call(s32[32,512]{1,0:T(8,128)} %bitcast.15, s32[1,32]{1,0:T(1,128)} %scnt.1, s32[4,64]{1,0:T(4,128)} %bitcast.16, s32[1,64]{1,0:T(1,128)} %lcnt.1, s32[4,64]{1,0:T(4,128)} %bitcast.17, s32[1,64]{1,0:T(1,128)} %hcnt.1, bf16[64,128,256]{2,1,0:T(8,128)(2,1)} %bitcast.14, ...), custom_call_target="tpu_custom_call" | custom-call | tf_op jit(solution)/shard_map/layer/pallas_call | solution.py:633
  189.0 2.0 %copy.15 = bf16[8192,256]{1,0:T(8,128)(2,1)} copy(bf16[8192,256]{1,0:T(8,128)(2,1)S(1)} %bitcast.11) | data formatting | bytes 8388608
  191.0 0.6 copy.16
